TPU v7x, 32 devices: a whole 2x2x4 slice. The times are simulated.
32 devices in a mesh: gx: 16 (over z, x, core), gy: 2 (over y).
Axes of the slice: x: 2, y: 2, z: 4, core: 2. Of those that a mesh axis runs over, the one named last changes fastest.
Arguments:
- volt: float32 [128, 128, 2048], P('gx', 'gy'), may hold values from -6 to 6
- drive: float32 [128, 128, 2048], P('gx', 'gy'), may hold values from -6 to 6
- region: int32 [128, 128, 32], P('gx', 'gy'), may hold values from 0 to 7
- diode_mask: int32 [128, 128, 32], P('gx', 'gy'), may hold values 0 or 1
- sigma_table: float32 [8], replicated, may hold values from 0.3 to 3
- cap_table: float32 [8], replicated, may hold values from 0.1 to 1
Outputs:
- residual: float32 [128, 128, 2048], P('gx', 'gy')
- coef_norms: float32 [64], replicated
All inputs are finite; a program needn't handle non-finite values. No bound on the sum of `diode_mask` on one device may be relied on, other than what follows from the above.
Results may differ from a plain program's by a relative error of at most 0.0003.
Values sent between devices are 32-bit elements; how exact they have to be, the bound alone decides.
A program may use at most 192 MiB of HBM per device.

v0:
```python
import math

import jax
import jax.numpy as jnp
from jax import lax
from jax.sharding import PartitionSpec as P

NZ = 32
H = 32
KC = 64
S = 256


base_freq = 0.1
norm_eps = 1e-06


def padded_2(block, sides, width, periodic):
    for axis, dim in sides:
        count = lax.axis_size(axis)
        forward = [(i, i + 1) for i in range(count - 1)]
        if periodic:
            forward.append((count - 1, 0))
        backward = [(target, source) for source, target in forward]
        low = lax.ppermute(
            lax.slice_in_dim(block, block.shape[dim] - width, None, axis=dim), axis, forward
        )
        high = lax.ppermute(lax.slice_in_dim(block, 0, width, axis=dim), axis, backward)
        block = jnp.concatenate([low, block, high], axis=dim)
    return block


def cut_slab(array, first_idx, last_idx, along):
    return lax.slice_in_dim(array, first_idx, last_idx, axis=along)


def harmonic_mean(left, right):
    return 2.0 * left * right / (left + right)


def open_terms(volt_field, conduct, along):
    cell_count = volt_field.shape[along]
    widths = [(0, 0)] * volt_field.ndim
    widths[along] = (1, 1)
    padded_volt = jnp.pad(volt_field, widths)
    padded_cond = jnp.pad(conduct, widths)
    face_flux = harmonic_mean(
        cut_slab(padded_cond, 0, cell_count + 1, along),
        cut_slab(padded_cond, 1, cell_count + 2, along),
    ) * (
        cut_slab(padded_volt, 1, cell_count + 2, along)
        - cut_slab(padded_volt, 0, cell_count + 1, along)
    )
    return cut_slab(face_flux, 0, cell_count, along) - cut_slab(face_flux, 1, cell_count + 1, along)


def time_derivative(coefs):
    half_count = coefs.shape[-1] // 2
    orders = base_freq * jnp.arange(1, half_count + 1, dtype=jnp.float32)
    return jnp.concatenate(
        [orders * coefs[..., half_count:], -orders * coefs[..., :half_count]], axis=-1
    )


def spectral_tables(harmonics, samples):
    orders = jnp.arange(1, harmonics + 1, dtype=jnp.float32)
    times = 2.0 * math.pi * jnp.arange(samples, dtype=jnp.float32) / samples
    angles = orders[:, None] * times[None, :]
    synthesis = jnp.concatenate([jnp.cos(angles), jnp.sin(angles)], axis=0)
    analysis = synthesis.T * (2.0 / samples)
    return (synthesis, analysis)


def nonlinear_row(volt_row, diode_row, synthesis, analysis):
    coef_count = volt_row.shape[-1]
    flat = volt_row.reshape(-1, coef_count)
    cell_count = flat.shape[0]
    samples = jnp.dot(
        flat, synthesis, precision=lax.Precision.HIGHEST, preferred_element_type=jnp.float32
    )
    current = jax.nn.softplus(2.0 * samples) * 0.5
    charge = jnp.tanh(samples) * 0.5
    projected = jnp.dot(
        jnp.concatenate([current, charge], axis=0),
        analysis,
        precision=lax.Precision.HIGHEST,
        preferred_element_type=jnp.float32,
    )
    combined = projected[:cell_count] + time_derivative(projected[cell_count:])
    return combined.reshape(volt_row.shape) * diode_row[..., None]


def lookup(region, region_table):
    onehot = (region[..., None] == jnp.arange(region_table.shape[0], dtype=jnp.int32)).astype(
        jnp.float32
    )
    return jnp.sum(onehot * region_table, axis=-1)


def unpack(packed_block):
    row_width = NZ * KC
    volt_part = packed_block[..., :row_width].reshape(packed_block.shape[:-1] + (NZ, KC))
    cond_part = packed_block[..., row_width : row_width + NZ][..., None]
    return (volt_part, cond_part)


def edge_flux(low_block, high_block):
    low_volt, low_cond = unpack(low_block)
    high_volt, high_cond = unpack(high_block)
    return harmonic_mean(low_cond, high_cond) * (high_volt - low_volt)


def face_terms_both(padded, along, cell_count):
    face_flux = edge_flux(
        cut_slab(padded, 0, cell_count + 1, along), cut_slab(padded, 1, cell_count + 2, along)
    )
    return cut_slab(face_flux, 0, cell_count, along) - cut_slab(face_flux, 1, cell_count + 1, along)


def body(volt, drive, region, diode_mask, sigma_table, cap_table):
    rows_local, cols_local, row_width = volt.shape
    conduct = lookup(region, sigma_table)
    capacity = lookup(region, cap_table)[..., None]
    padding = jnp.zeros((rows_local, cols_local, 128 - NZ), jnp.float32)
    packed = jnp.concatenate([volt, conduct, padding], axis=2)
    volt_field = volt.reshape(rows_local, cols_local, NZ, KC)
    padded_rows = padded_2(packed, (("gx", 0),), 1, True)
    row_terms = face_terms_both(padded_rows, 0, rows_local)
    padded_cols = padded_2(packed, (("gy", 1),), 1, False)
    col_terms = face_terms_both(padded_cols, 1, cols_local)
    depth_terms = open_terms(volt_field, conduct[..., None], 2)
    synthesis, analysis = spectral_tables(H, S)
    diode_field = diode_mask.astype(jnp.float32)

    def diode_rows(pair):
        return nonlinear_row(pair[0], pair[1], synthesis, analysis)

    diode_part = lax.map(diode_rows, (volt_field, diode_field))
    drive_field = drive.reshape(rows_local, cols_local, NZ, KC)
    residual = (
        row_terms
        + col_terms
        + depth_terms
        + capacity * time_derivative(volt_field)
        + diode_part
        - drive_field
    )
    partial_value = jnp.sum(residual * residual, axis=(0, 1, 2))
    summed = lax.psum(partial_value, ("gx", "gy"))
    cells_total = rows_local * cols_local * NZ * lax.axis_size("gx") * lax.axis_size("gy")
    norms_out = jnp.sqrt(summed / cells_total + norm_eps)
    return (residual.reshape(rows_local, cols_local, row_width), norms_out)


def solution(mesh):
    return jax.shard_map(
        body,
        mesh=mesh,
        in_specs=(
            P("gx", "gy", None),
            P("gx", "gy", None),
            P("gx", "gy", None),
            P("gx", "gy", None),
            P(),
            P(),
        ),
        out_specs=(P("gx", "gy", None), P()),
        check_vma=False,
    )
```

profile of v0, /device:TPU:0, one launch (start us, length us, event | category | flops | bytes accessed | tf_op | source)
XLA Modules:
  0.0 276.8 jit_solution(9313715618843078613)
XLA Ops:
  2.4 5.9 %concatenate.29 = f32[8,64,2176]{2,1,0:T(8,128)} concatenate(f32[8,64,2048]{2,1,0:T(8,128)} %param.8, f32[8,64,32]{2,1,0:T(8,128)S(1)} %copy.52, f32[8,64,96]{2,1,0:T(8,128)S(1)} %broadcast_in_dim.7), dimensions={2} | concatenate | bytes 8912896 | tf_op jit(solution)/shard_map/concatenate | solution.py:125
  11.2 5.0 %collective-permute-start.1 = (f32[1,64,2176]{2,1,0:T(8,128)}, f32[1,64,2176]{2,1,0:T(8,128)S(1)}, u32[]{:S(2)}, u32[]{:S(2)}) collective-permute-start(f32[1,64,2176]{2,1,0:T(8,128)} %get-tuple-element.71), channel_id=1, source_target_pairs={{2,0},{4,2},{6,4},{8,6},{10,8},{12,10},{14,12},{16,14},{18,16},{20... | collective-permute-start | bytes 1671176 | tf_op jit(solution)/shard_map/ppermute | solution.py:28
  17.5 3.9 %collective-permute-start.2 = (f32[8,1,2176]{2,0,1:T(8,128)S(1)}, f32[8,1,2176]{2,0,1:T(8,128)S(1)}, u32[]{:S(2)}, u32[]{:S(2)}) collective-permute-start(f32[8,1,2176]{2,0,1:T(8,128)S(1)} %copy.53), channel_id=1, source_target_pairs={{0,1},{2,3},{4,5},{6,7},{8,9},{10,11},{12,13},{14,15},{16,17},{18,... | collective-permute-start | bytes 208904 | tf_op jit(solution)/shard_map/ppermute | solution.py:25
  22.7 7.9 %reshape.76 = f32[8,64,32,64]{3,2,1,0:T(8,128)} reshape(f32[8,64,2048]{2,1,0:T(8,128)} %param.8) | data formatting | bytes 8388608 | tf_op jit(solution)/shard_map/reshape | solution.py:126
  32.2 90.9 %while.10 = (s32[]{:T(128)}, f32[8,64,32,64]{3,2,1,0:T(8,128)}, f32[8,64,32,64]{3,2,1,0:T(8,128)}, f32[64,256]{1,0:T(8,128)}, f32[256,64]{1,0:T(8,128)S(1)}, /*index=5*/f32[8,64,32]{2,1,0:T(8,128)S(1)}, s32[]{:T(128)}) while((s32[]{:T(128)}, f32[8,64,32,64]{3,2,1,0:T(8,128)}, f32[8,64,32,64]{3,2,1,0:T(8,128)}, f32[64,256]{1,0:T(8,128)}, ...), condition=%wide.region_3.4_spmd, body=%wide.region_2.3_spmd.sunk | while | flops 1214251136 | bytes 16409685 | solution.py:138
  33.5 3.9 %fusion.33 = (f32[2048,256]{1,0:T(8,128)S(1)}, f32[2048,256]{1,0:T(8,128)S(1)}) fusion(f32[2048,64]{1,0:T(8,128)S(1)} %bitcast.31, f32[64,256]{1,0:T(8,128)} %get-tuple-element.147), kind=kOutput, calls=%fused_computation.5.clone.1 | convolution fusion | flops 407371776 | bytes 4784128 | tf_op jit(solution)/shard_map/while/body/eval_jaxpr/dot_general | solution.py:78
  37.4 4.2 %fusion.34 = f32[4096,64]{0,1:T(8,128)S(1)} fusion(f32[256,64]{1,0:T(8,128)S(1)} %get-tuple-element.148, f32[2048,256]{1,0:T(8,128)S(1)} %get-tuple-element.124, f32[2048,256]{1,0:T(8,128)S(1)} %get-tuple-element.125), kind=kOutput, calls=%fused_computation.1.clone.1 | convolution fusion | flops 806354944 | bytes 5308416 | tf_op jit(solution)/shard_map/while/body/eval_jaxpr/dot_general | solution.py:83
  44.9 3.9 %fusion.33 = (f32[2048,256]{1,0:T(8,128)S(1)}, f32[2048,256]{1,0:T(8,128)S(1)}) fusion(f32[2048,64]{1,0:T(8,128)S(1)} %bitcast.31, f32[64,256]{1,0:T(8,128)} %get-tuple-element.147), kind=kOutput, calls=%fused_computation.5.clone.1 | convolution fusion | flops 407371776 | bytes 4784128 | tf_op jit(solution)/shard_map/while/body/eval_jaxpr/dot_general | solution.py:78
  48.8 4.2 %fusion.34 = f32[4096,64]{0,1:T(8,128)S(1)} fusion(f32[256,64]{1,0:T(8,128)S(1)} %get-tuple-element.148, f32[2048,256]{1,0:T(8,128)S(1)} %get-tuple-element.124, f32[2048,256]{1,0:T(8,128)S(1)} %get-tuple-element.125), kind=kOutput, calls=%fused_computation.1.clone.1 | convolution fusion | flops 806354944 | bytes 5308416 | tf_op jit(solution)/shard_map/while/body/eval_jaxpr/dot_general | solution.py:83
  56.2 3.9 %fusion.33 = (f32[2048,256]{1,0:T(8,128)S(1)}, f32[2048,256]{1,0:T(8,128)S(1)}) fusion(f32[2048,64]{1,0:T(8,128)S(1)} %bitcast.31, f32[64,256]{1,0:T(8,128)} %get-tuple-element.147), kind=kOutput, calls=%fused_computation.5.clone.1 | convolution fusion | flops 407371776 | bytes 4784128 | tf_op jit(solution)/shard_map/while/body/eval_jaxpr/dot_general | solution.py:78
  60.1 4.2 %fusion.34 = f32[4096,64]{0,1:T(8,128)S(1)} fusion(f32[256,64]{1,0:T(8,128)S(1)} %get-tuple-element.148, f32[2048,256]{1,0:T(8,128)S(1)} %get-tuple-element.124, f32[2048,256]{1,0:T(8,128)S(1)} %get-tuple-element.125), kind=kOutput, calls=%fused_computation.1.clone.1 | convolution fusion | flops 806354944 | bytes 5308416 | tf_op jit(solution)/shard_map/while/body/eval_jaxpr/dot_general | solution.py:83
  67.5 3.9 %fusion.33 = (f32[2048,256]{1,0:T(8,128)S(1)}, f32[2048,256]{1,0:T(8,128)S(1)}) fusion(f32[2048,64]{1,0:T(8,128)S(1)} %bitcast.31, f32[64,256]{1,0:T(8,128)} %get-tuple-element.147), kind=kOutput, calls=%fused_computation.5.clone.1 | convolution fusion | flops 407371776 | bytes 4784128 | tf_op jit(solution)/shard_map/while/body/eval_jaxpr/dot_general | solution.py:78
  71.5 4.2 %fusion.34 = f32[4096,64]{0,1:T(8,128)S(1)} fusion(f32[256,64]{1,0:T(8,128)S(1)} %get-tuple-element.148, f32[2048,256]{1,0:T(8,128)S(1)} %get-tuple-element.124, f32[2048,256]{1,0:T(8,128)S(1)} %get-tuple-element.125), kind=kOutput, calls=%fused_computation.1.clone.1 | convolution fusion | flops 806354944 | bytes 5308416 | tf_op jit(solution)/shard_map/while/body/eval_jaxpr/dot_general | solution.py:83
  78.9 3.9 %fusion.33 = (f32[2048,256]{1,0:T(8,128)S(1)}, f32[2048,256]{1,0:T(8,128)S(1)}) fusion(f32[2048,64]{1,0:T(8,128)S(1)} %bitcast.31, f32[64,256]{1,0:T(8,128)} %get-tuple-element.147), kind=kOutput, calls=%fused_computation.5.clone.1 | convolution fusion | flops 407371776 | bytes 4784128 | tf_op jit(solution)/shard_map/while/body/eval_jaxpr/dot_general | solution.py:78
  82.8 4.2 %fusion.34 = f32[4096,64]{0,1:T(8,128)S(1)} fusion(f32[256,64]{1,0:T(8,128)S(1)} %get-tuple-element.148, f32[2048,256]{1,0:T(8,128)S(1)} %get-tuple-element.124, f32[2048,256]{1,0:T(8,128)S(1)} %get-tuple-element.125), kind=kOutput, calls=%fused_computation.1.clone.1 | convolution fusion | flops 806354944 | bytes 5308416 | tf_op jit(solution)/shard_map/while/body/eval_jaxpr/dot_general | solution.py:83
  90.3 3.9 %fusion.33 = (f32[2048,256]{1,0:T(8,128)S(1)}, f32[2048,256]{1,0:T(8,128)S(1)}) fusion(f32[2048,64]{1,0:T(8,128)S(1)} %bitcast.31, f32[64,256]{1,0:T(8,128)} %get-tuple-element.147), kind=kOutput, calls=%fused_computation.5.clone.1 | convolution fusion | flops 407371776 | bytes 4784128 | tf_op jit(solution)/shard_map/while/body/eval_jaxpr/dot_general | solution.py:78
  94.2 4.2 %fusion.34 = f32[4096,64]{0,1:T(8,128)S(1)} fusion(f32[256,64]{1,0:T(8,128)S(1)} %get-tuple-element.148, f32[2048,256]{1,0:T(8,128)S(1)} %get-tuple-element.124, f32[2048,256]{1,0:T(8,128)S(1)} %get-tuple-element.125), kind=kOutput, calls=%fused_computation.1.clone.1 | convolution fusion | flops 806354944 | bytes 5308416 | tf_op jit(solution)/shard_map/while/body/eval_jaxpr/dot_general | solution.py:83
  101.6 3.9 %fusion.33 = (f32[2048,256]{1,0:T(8,128)S(1)}, f32[2048,256]{1,0:T(8,128)S(1)}) fusion(f32[2048,64]{1,0:T(8,128)S(1)} %bitcast.31, f32[64,256]{1,0:T(8,128)} %get-tuple-element.147), kind=kOutput, calls=%fused_computation.5.clone.1 | convolution fusion | flops 407371776 | bytes 4784128 | tf_op jit(solution)/shard_map/while/body/eval_jaxpr/dot_general | solution.py:78
  105.6 4.2 %fusion.34 = f32[4096,64]{0,1:T(8,128)S(1)} fusion(f32[256,64]{1,0:T(8,128)S(1)} %get-tuple-element.148, f32[2048,256]{1,0:T(8,128)S(1)} %get-tuple-element.124, f32[2048,256]{1,0:T(8,128)S(1)} %get-tuple-element.125), kind=kOutput, calls=%fused_computation.1.clone.1 | convolution fusion | flops 806354944 | bytes 5308416 | tf_op jit(solution)/shard_map/while/body/eval_jaxpr/dot_general | solution.py:83
  113.0 3.9 %fusion.33 = (f32[2048,256]{1,0:T(8,128)S(1)}, f32[2048,256]{1,0:T(8,128)S(1)}) fusion(f32[2048,64]{1,0:T(8,128)S(1)} %bitcast.31, f32[64,256]{1,0:T(8,128)} %get-tuple-element.147), kind=kOutput, calls=%fused_computation.5.clone.1 | convolution fusion | flops 407371776 | bytes 4784128 | tf_op jit(solution)/shard_map/while/body/eval_jaxpr/dot_general | solution.py:78
  116.9 4.2 %fusion.34 = f32[4096,64]{0,1:T(8,128)S(1)} fusion(f32[256,64]{1,0:T(8,128)S(1)} %get-tuple-element.148, f32[2048,256]{1,0:T(8,128)S(1)} %get-tuple-element.124, f32[2048,256]{1,0:T(8,128)S(1)} %get-tuple-element.125), kind=kOutput, calls=%fused_computation.1.clone.1 | convolution fusion | flops 806354944 | bytes 5308416 | tf_op jit(solution)/shard_map/while/body/eval_jaxpr/dot_general | solution.py:83
  123.2 13.1 %slice_multiply_fusion.3 = (f32[8,64,32,32]{3,2,1,0:T(8,128)}, f32[8,64,32,32]{3,2,1,0:T(8,128)}) fusion(f32[8,64,32,64]{3,2,1,0:T(8,128)} %get-tuple-element.151, f32[32]{0:T(128)S(1)} %get-tuple-element.79, f32[32]{0:T(128)} %get-tuple-element.80), kind=kLoop, calls=%fused_computation.21 | loop fusion | flops 1048576 | bytes 8388864 | tf_op jit(solution)/shard_map/mul | solution.py:61
  136.3 6.8 %fusion.8 = f32[8,64,33,64]{3,2,1,0:T(8,128)} fusion(f32[8,64,32,64]{3,2,1,0:T(8,128)S(1)} %copy-done, f32[8,64,33]{2,1,0:T(8,128)S(1)} %copy.59), kind=kLoop, calls=%fused_computation.19 | loop fusion | flops 2162688 | bytes 8587264 | tf_op jit(solution)/shard_map/mul | solution.py:47
  143.2 7.8 %reshape.77 = f32[8,64,32,64]{3,2,1,0:T(8,128)} reshape(f32[8,64,2048]{2,1,0:T(8,128)} %param.9) | data formatting | bytes 8388608 | tf_op jit(solution)/shard_map/reshape | solution.py:139
  152.3 7.3 %fusion.14 = f32[8,65,2048]{2,1,0:T(8,128)} fusion(f32[8,64,2176]{2,1,0:T(8,128)} %concatenate.29, f32[8,1,2176]{2,1,0:T(1,128)S(1)} %copy.54, f32[8,1,2176]{2,1,0:T(1,128)S(1)} %copy.56), kind=kLoop, calls=%fused_computation.33 | loop fusion | flops 3194880 | bytes 8855552 | tf_op jit(solution)/shard_map/sub | solution.py:110
  159.6 7.6 %reshape.79 = f32[8,65,32,64]{3,2,1,0:T(8,128)} reshape(f32[8,65,2048]{2,1,0:T(8,128)} %fusion.14) | data formatting | bytes 8519680 | tf_op jit(solution)/shard_map/sub | solution.py:110
  167.3 8.4 %broadcast_multiply_fusion.1 = f32[8,65,32,64]{3,2,1,0:T(8,128)} fusion(f32[8,65,32,64]{3,2,1,0:T(8,128)} %reshape.79, f32[8,65,32]{2,1,0:T(8,128)S(1)} %add_divide_fusion), kind=kLoop, calls=%fused_computation.39 | loop fusion | flops 1064960 | bytes 8586240 | tf_op jit(solution)/shard_map/mul | solution.py:110
  178.5 8.7 %sub.28 = f32[9,64,32,64]{3,2,1,0:T(8,128)} reshape(f32[9,64,2048]{2,1,0:T(8,128)} %fusion.15) | data formatting | bytes 9437184 | tf_op jit(solution)/shard_map/sub | solution.py:110
  188.3 8.8 %broadcast_multiply_fusion = f32[9,64,32,64]{3,2,1,0:T(8,128)} fusion(f32[9,64,32,64]{3,2,1,0:T(8,128)} %sub.28, f32[9,64,32]{2,1,0:T(8,128)S(1)} %add_divide_fusion.1), kind=kLoop, calls=%fused_computation.38 | loop fusion | flops 1179648 | bytes 9510912 | tf_op jit(solution)/shard_map/mul | solution.py:110
  197.1 31.9 %multiply_reduce_fusion = (f32[64]{0:T(128)S(1)}, f32[8,64,32,64]{3,2,1,0:T(8,128)}) fusion(f32[8,64,32,64]{3,2,1,0:T(8,128)} %reshape.77, f32[8,64,32,64]{3,2,1,0:T(8,128)} %get-tuple-element.34, f32[8,64,32,32]{3,2,1,0:T(8,128)} %get-tuple-element.70, f32[8,64,32,32]{3,2,1,0:T(8,128)} %get-tuple-element.69, f32[8,64,32]{2,1,0:T(8,128)S(1)} %copy.60, ...), kind=kLoop, calls=%fused_computation.31 | loop fusion | flops 12582848 | bytes 42008832 | tf_op jit(solution)/shard_map/reduce_sum | solution.py:148
  229.0 7.8 %reshape.78 = f32[8,64,2048]{2,1,0:T(8,128)} reshape(f32[8,64,32,64]{3,2,1,0:T(8,128)} %get-tuple-element.62) | data formatting | bytes 8388608 | tf_op jit(solution)/shard_map/reshape | solution.py:152
  236.8 39.5 %psum.7 = f32[64]{0:T(128)S(1)} all-reduce(f32[64]{0:T(128)S(1)} %get-tuple-element.61), channel_id=1, replica_groups=mesh['gx'=16,'gy'=2] {'gx','gy'}, use_global_device_ids=true, to_apply=%region_5.6 | all-reduce | flops 64 | bytes 512 | tf_op jit(solution)/shard_map/psum | solution.py:149
  (101 shorter events, 40.1 us)
Async XLA Ops:
  8.3 23.6 %copy-start.1 = (s32[8,64,32]{1,2,0:T(8,128)S(1)}, s32[8,64,32]{1,2,0:T(8,128)}, u32[]{:S(2)}) copy-start(s32[8,64,32]{1,2,0:T(8,128)} %param.11) | copy-start | bytes 196612
  10.7 165.0 %collective-permute-start = (f32[1,64,2176]{2,1,0:T(8,128)}, f32[1,64,2176]{2,1,0:T(8,128)S(1)}, u32[]{:S(2)}, u32[]{:S(2)}) collective-permute-start(f32[1,64,2176]{2,1,0:T(8,128)} %get-tuple-element.72), channel_id=1, source_target_pairs={{0,2},{2,4},{4,6},{6,8},{8,10},{10,12},{12,14},{14,16},{16,18},{18... | collective-permute-start | bytes 1671176 | tf_op jit(solution)/shard_map/ppermute | solution.py:25
  11.2 164.5 %collective-permute-start.1 = (f32[1,64,2176]{2,1,0:T(8,128)}, f32[1,64,2176]{2,1,0:T(8,128)S(1)}, u32[]{:S(2)}, u32[]{:S(2)}) collective-permute-start(f32[1,64,2176]{2,1,0:T(8,128)} %get-tuple-element.71), channel_id=1, source_target_pairs={{2,0},{4,2},{6,4},{8,6},{10,8},{12,10},{14,12},{16,14},{18,16},{20... | collective-permute-start | bytes 1671176 | tf_op jit(solution)/shard_map/ppermute | solution.py:28
  17.5 133.6 %collective-permute-start.2 = (f32[8,1,2176]{2,0,1:T(8,128)S(1)}, f32[8,1,2176]{2,0,1:T(8,128)S(1)}, u32[]{:S(2)}, u32[]{:S(2)}) collective-permute-start(f32[8,1,2176]{2,0,1:T(8,128)S(1)} %copy.53), channel_id=1, source_target_pairs={{0,1},{2,3},{4,5},{6,7},{8,9},{10,11},{12,13},{14,15},{16,17},{18,... | collective-permute-start | bytes 208904 | tf_op jit(solution)/shard_map/ppermute | solution.py:25
  21.4 129.7 %collective-permute-start.3 = (f32[8,1,2176]{2,0,1:T(8,128)S(1)}, f32[8,1,2176]{2,0,1:T(8,128)}, u32[]{:S(2)}, u32[]{:S(2)}) collective-permute-start(f32[8,1,2176]{2,0,1:T(8,128)S(1)} %copy.55), channel_id=1, source_target_pairs={{1,0},{3,2},{5,4},{7,6},{9,8},{11,10},{13,12},{15,14},{17,16},{19,... | collective-permute-start | bytes 208904 | tf_op jit(solution)/shard_map/ppermute | solution.py:28
  123.2 13.1 %copy-start = (f32[8,64,32,64]{3,2,1,0:T(8,128)S(1)}, f32[8,64,32,64]{3,2,1,0:T(8,128)}, u32[]{:S(2)}) copy-start(f32[8,64,32,64]{3,2,1,0:T(8,128)} %get-tuple-element.151) | copy-start | bytes 12582916
  151.0 8.5 %slice-start = ((s8[4456448]{0:T(1024)(128)(4,1)}), s8[4194304]{0:T(1024)(128)(4,1)S(1)}, s32[]{:S(2)}) async-start(s8[4456448]{0:T(1024)(128)(4,1)} %bitcast.26), calls=%async_computation | async-start | bytes 8388608
  152.2 7.3 %slice-start.1 = ((s8[4456448]{0:T(1024)(128)(4,1)}), s8[262144]{0:T(1024)(128)(4,1)S(1)}, s32[]{:S(2)}) async-start(s8[4456448]{0:T(1024)(128)(4,1)} %bitcast.26), calls=%async_computation.1 | async-start | bytes 524288
  159.6 16.0 %slice-start.2 = ((s8[4456448]{0:T(1024)(128)(4,1)}), s8[262144]{0:T(1024)(128)(4,1)S(1)}, s32[]{:S(2)}) async-start(s8[4456448]{0:T(1024)(128)(4,1)} %bitcast.28), calls=%async_computation.2 | async-start | bytes 524288
  167.3 8.4 %slice-start.3 = ((s8[4456448]{0:T(1024)(128)(4,1)}), s8[4194304]{0:T(1024)(128)(4,1)S(1)}, s32[]{:S(2)}) async-start(s8[4456448]{0:T(1024)(128)(4,1)} %bitcast.28), calls=%async_computation.3 | async-start | bytes 8388608
where the time goes:
time: 279 us; the launch traced here: 277 us
  other arithmetic  95.9 us (34%)
  matrix products  65.3 us (23%)
  local copies, waits for them, and re-layouts  64.3 us (23%)
  blocking collectives  39.5 us (14%)
  starting transfers between devices  10.6 us (4%)
    psum x1, blocking collectives, body(): summed = lax.psum(partial_value, ('gx', 'gy'))  39.5 us
    dot_general x8, matrix products, nonlinear_row(): jnp.dot(jnp.concatenate([current, charge], axis=0), analysis, precision=l...  34 us
    reduce_sum x1, other arithmetic, body(): partial_value = jnp.sum(residual * residual, axis=(0, 1, 2))  31.9 us
    dot_general x8, matrix products, nonlinear_row(): jnp.dot(flat, synthesis, precision=lax.Precision.HIGHEST, preferred_eleme...  31.3 us
    mul x2, other arithmetic, edge_flux(): return harmonic_mean(low_cond, high_cond) * (high_volt - low_volt)  17.2 us
    sub x2, local copies, waits for them, and re-layouts, edge_flux(): return harmonic_mean(low_cond, high_cond) * (high_volt - low_volt)  16.4 us
    mul x9, other arithmetic, time_derivative(): orders * coefs[..., half_count:]  13.9 us
    dynamic_update_slice x8, other arithmetic, body(): diode_part = lax.map(diode_rows, (volt_field, diode_field))  10.7 us
  transfers between devices with their start and end apart: 4, of which 0 were waited for; matrix products, arithmetic and copies ran while one was open for 56% of the time, Pallas kernels for 0%

commit v1 on v0

v1 whole, which is shorter than its diff:
```python
import functools
import math

import jax
import jax.numpy as jnp
import numpy as np
from jax import lax
from jax.experimental import pallas as pl
from jax.experimental.pallas import tpu as pltpu
from jax.sharding import PartitionSpec as P

NZ = 32
H = 32
KC = 64
S = 256
LANES = 128
TILES = NZ * KC // LANES
CHUNK = 8

base_freq = 0.1
norm_eps = 1e-06


def tables():
    orders = np.arange(1, H + 1, dtype=np.float64)
    angles = orders[:, None] * (2.0 * math.pi * np.arange(S) / S)[None, :]
    synthesis = np.concatenate([np.cos(angles), np.sin(angles)], axis=0)
    analysis = synthesis.T * (2.0 / S)
    derived = np.concatenate(
        [base_freq * orders * analysis[:, H:], -base_freq * orders * analysis[:, :H]], axis=1
    )

    def split(table):
        high = table.astype(jnp.bfloat16)
        low = (table - high.astype(np.float64)).astype(jnp.bfloat16)
        return high, low

    high, low = split(synthesis)
    forward = np.concatenate([high, high, low, low], axis=0)
    cell = 0.5 * np.concatenate([analysis, derived], axis=0)
    both = np.zeros((4 * S, LANES))
    both[: 2 * S, :KC] = cell
    both[2 * S :, KC:] = cell
    high, low = split(both)
    return jnp.asarray(forward), jnp.asarray(np.concatenate([high, low], axis=1))


def lookup(region, table, count):
    value = jnp.where(region == 0, table[0], 0.0)
    for r in range(1, count):
        value = jnp.where(region == r, table[r], value)
    return value


def harmonic_mean(left, right):
    return 2.0 * left * right / (left + right)


def spread(cells, tile, lane):
    index = 2 * tile + (lane >= KC).astype(jnp.int32)
    return jnp.take_along_axis(cells, index, axis=1, mode="promise_in_bounds")


def main_kernel(
    regions, rows, cols,
    volt_hbm, drive_ref, region_ref, mask_ref, left_ref, right_ref, sigma_ref, cap_ref,
    forward_ref, back_ref, out_ref, squares_ref,
    volt_buf, cond_buf, cell_buf, flux_buf, acc_ref, sems,
):
    i = pl.program_id(0)

    def copy(row):
        return pltpu.make_async_copy(volt_hbm.at[row], volt_buf.at[row], sems.at[row])

    @pl.when(i == 0)
    def _():
        for row in range(rows):
            copy(row).start()
        cond_buf[:, :, :NZ] = lookup(region_ref[...], sigma_ref, regions)
        acc_ref[...] = jnp.zeros_like(acc_ref)
        flux_buf[...] = jnp.zeros_like(flux_buf)
        copy(0).wait()

    @pl.when(i < rows - 1)
    def _():
        copy(i + 1).wait()

    after = jnp.minimum(i + 1, rows - 1)
    lane = lax.broadcasted_iota(jnp.int32, (cols, LANES), 1)
    col = lax.broadcasted_iota(jnp.int32, (cols, LANES), 0)
    cell_lane = lax.broadcasted_iota(jnp.int32, (cols, LANES), 1)
    cond = jnp.where(cell_lane < NZ, cond_buf[i], 1.0)
    cond_next = jnp.where(cell_lane < NZ, cond_buf[after], 1.0)
    width = NZ * KC
    edge_left = left_ref[0, :, width : width + LANES]
    edge_right = right_ref[0, :, width : width + LANES]
    g_row = jnp.where(i < rows - 1, harmonic_mean(cond, cond_next), 0.0)
    cond_after = jnp.where(
        col == cols - 1, jnp.broadcast_to(edge_right, cond.shape), pltpu.roll(cond, cols - 1, 0)
    )
    g_col = harmonic_mean(cond, cond_after)
    g_left = harmonic_mean(cond, jnp.broadcast_to(edge_left, cond.shape))
    g_depth = jnp.where(
        cell_lane < NZ - 1, harmonic_mean(cond, pltpu.roll(cond, LANES - 1, 1)), 0.0
    )
    cell_buf[0, :, :NZ] = lookup(region_ref[i], cap_ref, regions)
    cell_buf[1, :, :NZ] = mask_ref[i].astype(jnp.float32)
    capacity = cell_buf[0]
    diode = cell_buf[1]

    first = lane < KC
    half = lane % KC
    order = base_freq * (half % H + 1).astype(jnp.float32)
    order = jnp.where(half < H, order, -order)
    swap = lane ^ H

    def tile_of(ref_value, t):
        return ref_value[:, t * LANES : (t + 1) * LANES]

    turned_next = None
    prev_flux = None
    total = jnp.zeros((8, LANES), jnp.float32)
    for start in range(0, TILES, CHUNK):
        xa, xb, turned = [], [], []
        for t in range(start, start + CHUNK):
            v = volt_buf[i, :, t * LANES : (t + 1) * LANES]
            high = v.astype(jnp.bfloat16).astype(jnp.float32)
            low = v - high
            high_r = pltpu.roll(high, KC, 1)
            low_r = pltpu.roll(low, KC, 1)
            xa.append(jnp.where(first, high, low_r).astype(jnp.bfloat16))
            xb.append(jnp.where(first, high_r, low).astype(jnp.bfloat16))
            turned.append(high_r + low_r)
        if start + CHUNK < TILES:
            t = start + CHUNK
            turned.append(pltpu.roll(volt_buf[i, :, t * LANES : (t + 1) * LANES], KC, 1))
        else:
            turned.append(turned[-1])
        x = jnp.concatenate(xa + xb, axis=0)
        samples = jnp.dot(
            jnp.concatenate([x, x], axis=1), forward_ref[...], preferred_element_type=jnp.float32
        )
        size = jnp.abs(samples)
        small = jnp.exp2(size * (-2.0 / math.log(2.0)) - 1.0)
        even = (size + jnp.log(0.5 + small)).astype(jnp.bfloat16)
        charge = jnp.tanh(samples.astype(jnp.bfloat16))
        m = CHUNK * cols
        waves = jnp.concatenate([even[:m], charge[:m], even[m:], charge[m:]], axis=1)
        projected = jnp.dot(waves, back_ref[...], preferred_element_type=jnp.float32)
        projected = projected[:, :LANES] + projected[:, LANES:]
        for t in range(start, start + CHUNK):
            at = slice(t * LANES, (t + 1) * LANES)
            v = volt_buf[i, :, at]
            row_flux = spread(g_row, t, lane) * (volt_buf[after, :, at] - v)
            value = flux_buf[:, at] - row_flux
            flux_buf[:, at] = row_flux
            v_after = jnp.where(
                col == cols - 1,
                jnp.broadcast_to(right_ref[0, :, at], v.shape),
                pltpu.roll(v, cols - 1, 0),
            )
            col_flux = spread(g_col, t, lane) * (v_after - v)
            left_flux = spread(g_left[:8], t, lane[:8]) * (
                v[:8] - jnp.broadcast_to(left_ref[0, :, at], (8, LANES))
            )
            left_flux = jnp.concatenate([left_flux] * (cols // 8), axis=0)
            value += jnp.where(col == 0, left_flux, pltpu.roll(col_flux, 1, 0)) - col_flux
            v_deep = jnp.where(first, turned[t - start], turned[t - start + 1])
            deep_flux = spread(g_depth, t, lane) * (v_deep - v)
            deep_r = pltpu.roll(deep_flux, KC, 1)
            before = jnp.zeros_like(deep_r) if prev_flux is None else prev_flux
            value += jnp.where(first, before, deep_r) - deep_flux
            prev_flux = deep_r
            swapped = jnp.take_along_axis(v, swap, axis=1, mode="promise_in_bounds")
            value += spread(capacity, t, lane) * (order * swapped)
            rows_of = slice((t - start) * cols, (t - start + 1) * cols)
            value += spread(diode, t, lane) * (projected[rows_of] + 0.5 * v)
            value -= drive_ref[0, :, at]
            out_ref[0, :, at] = value
            total += jnp.sum((value * value).reshape(cols // 8, 8, LANES), axis=0)
    acc_ref[...] += total

    @pl.when(i == rows - 1)
    def _():
        squares_ref[...] = acc_ref[...]


def edge_kernel(
    last_row, width, part_ref, volt_ref, cond_ref, low_ref, high_ref, squares_ref,
    out_ref, sum_ref, acc_ref,
):
    side, step = pl.program_id(0), pl.program_id(1)

    @pl.when((side == 0) & (step == 0))
    def _():
        acc_ref[...] = squares_ref[...]

    cols = volt_ref.shape[1]
    lane = lax.broadcasted_iota(jnp.int32, (cols, LANES), 1)

    def fix(halo_ref):
        g = harmonic_mean(cond_ref[0], halo_ref[0, :, width : width + LANES])
        total = jnp.zeros((8, LANES), jnp.float32)
        for t in range(TILES):
            at = slice(t * LANES, (t + 1) * LANES)
            old = part_ref[0, :, at]
            new = old + spread(g, t, lane) * (volt_ref[0, :, at] - halo_ref[0, :, at])
            out_ref[0, :, at] = new
            change = (new - old) * (new + old)
            total += jnp.sum(change.reshape(cols // 8, 8, LANES), axis=0)
        acc_ref[...] += total

    @pl.when(side == 0)
    def _():
        fix(low_ref)

    @pl.when(side == 1)
    def _():
        fix(high_ref)

    sum_ref[...] = acc_ref[...]


def shift(block, axis, periodic):
    count = lax.axis_size(axis)
    forward = [(k, k + 1) for k in range(count - 1)]
    if periodic:
        forward.append((count - 1, 0))
    backward = [(b, a) for a, b in forward]
    return (
        lambda top: lax.ppermute(top, axis, forward),
        lambda bottom: lax.ppermute(bottom, axis, backward),
    )


def body(volt, drive, region, diode_mask, sigma_table, cap_table):
    rows, cols, width = volt.shape
    regions = sigma_table.shape[0]

    def conduct_of(part):
        onehot = part[..., None] == jnp.arange(regions, dtype=jnp.int32)
        value = jnp.sum(jnp.where(onehot, sigma_table, 0.0), axis=-1)
        return jnp.pad(value, [(0, 0)] * (value.ndim - 1) + [(0, LANES - NZ)])

    def packed(volt_part, region_part):
        return jnp.concatenate([volt_part, conduct_of(region_part)], axis=-1)

    up, down = shift(None, "gx", True)
    rightward, leftward = shift(None, "gy", False)
    left = rightward(packed(volt[:, -1:], region[:, -1:]))
    right = leftward(packed(volt[:, :1], region[:, :1]))
    low = up(packed(volt[-1:], region[-1:]))
    high = down(packed(volt[:1], region[:1]))
    forward, back = tables()

    whole = lambda *shape: pl.BlockSpec(shape, lambda i: (0,) * len(shape))
    smem = pl.BlockSpec(memory_space=pltpu.SMEM)
    row_spec = pl.BlockSpec((1, cols, width), lambda i: (i, 0, 0))
    part, squares = pl.pallas_call(
        functools.partial(main_kernel, regions, rows, cols),
        grid=(rows,),
        out_shape=(
            jax.ShapeDtypeStruct(volt.shape, jnp.float32),
            jax.ShapeDtypeStruct((8, LANES), jnp.float32),
        ),
        in_specs=[
            pl.BlockSpec(memory_space=pl.ANY),
            row_spec,
            whole(rows, cols, NZ),
            whole(rows, cols, NZ),
            pl.BlockSpec((1, 1, width + LANES), lambda i: (i, 0, 0)),
            pl.BlockSpec((1, 1, width + LANES), lambda i: (i, 0, 0)),
            smem,
            smem,
            whole(*forward.shape),
            whole(*back.shape),
        ],
        out_specs=(row_spec, whole(8, LANES)),
        scratch_shapes=[
            pltpu.VMEM((rows, cols, width), jnp.float32),
            pltpu.VMEM((rows, cols, LANES), jnp.float32),
            pltpu.VMEM((2, cols, LANES), jnp.float32),
            pltpu.VMEM((cols, width), jnp.float32),
            pltpu.VMEM((8, LANES), jnp.float32),
            pltpu.SemaphoreType.DMA((rows,)),
        ],
        compiler_params=pltpu.CompilerParams(
            dimension_semantics=("arbitrary",), vmem_limit_bytes=50 * 2**20
        ),
        cost_estimate=pl.CostEstimate(
            flops=20_000_000_000, bytes_accessed=3 * volt.size * 4, transcendentals=0
        ),
        name="cells",
    )(volt, drive, region, diode_mask, left, right, sigma_table, cap_table, forward, back)

    ends = jnp.concatenate([region[:1], region[-1:]], axis=0)
    step_cols = min(cols, 16)
    steps = cols // step_cols
    row_map = lambda s, c: (s * (rows - 1), c, 0)
    residual, sums = pl.pallas_call(
        functools.partial(edge_kernel, rows - 1, width),
        grid=(2, steps),
        out_shape=(
            jax.ShapeDtypeStruct(volt.shape, jnp.float32),
            jax.ShapeDtypeStruct((8, LANES), jnp.float32),
        ),
        in_specs=[
            pl.BlockSpec((1, step_cols, width), row_map),
            pl.BlockSpec((1, step_cols, width), row_map),
            pl.BlockSpec((1, step_cols, LANES), lambda s, c: (s, c, 0)),
            pl.BlockSpec(
                (1, step_cols, width + LANES),
                lambda s, c: (0, jnp.where(s == 0, c, steps - 1), 0),
            ),
            pl.BlockSpec(
                (1, step_cols, width + LANES), lambda s, c: (0, jnp.where(s == 1, c, 0), 0)
            ),
            pl.BlockSpec((8, LANES), lambda s, c: (0, 0)),
        ],
        out_specs=(
            pl.BlockSpec((1, step_cols, width), row_map),
            pl.BlockSpec((8, LANES), lambda s, c: (0, 0)),
        ),
        scratch_shapes=[pltpu.VMEM((8, LANES), jnp.float32)],
        input_output_aliases={0: 0},
        compiler_params=pltpu.CompilerParams(
            dimension_semantics=("arbitrary", "arbitrary"), vmem_limit_bytes=16 * 2**20
        ),
        name="edges",
    )(part, volt, conduct_of(ends), low, high, squares)

    partial_value = jnp.sum(sums.reshape(-1, KC), axis=0)
    summed = lax.psum(partial_value, ("gx", "gy"))
    cells_total = rows * cols * NZ * lax.axis_size("gx") * lax.axis_size("gy")
    return residual, jnp.sqrt(summed / cells_total + norm_eps)


def solution(mesh):
    return jax.shard_map(
        body,
        mesh=mesh,
        in_specs=(
            P("gx", "gy", None),
            P("gx", "gy", None),
            P("gx", "gy", None),
            P("gx", "gy", None),
            P(),
            P(),
        ),
        out_specs=(P("gx", "gy", None), P()),
        check_vma=False,
    )
```

time: 279 us -> 93.5 us (0.34)
  other arithmetic: 95.9 us -> 3.74 us
  matrix products: 65.3 us -> 0 us
  local copies, waits for them, and re-layouts: 64.3 us -> 7.65 us
  Pallas kernels: 0 us -> 31.1 us
    dot_general x16 -> x0, matrix products: 65.3 us -> none  [the longest x8 34 us: nonlinear_row(): jnp.dot(jnp.concatenate([current, charge], axis=0), analysis, precision=l...]
    mul x23 -> x0, other arithmetic: 39.1 us -> none  [the longest x2 17.2 us: edge_flux(): return harmonic_mean(low_cond, high_cond) * (high_volt - low_volt)]
    reduce_sum x2 -> x4, other arithmetic: 33.5 us -> 1.75 us  [the longest x3 1.73 us: conduct_of(): value = jnp.sum(jnp.where(onehot, sigma_table, 0.0), axis=-1)]
    pallas_call x0 -> x2, Pallas kernels: none -> 31.1 us  [the longest x1 25.3 us: body(): pl.pallas_call(functools.partial(main_kernel, regions, rows, cols), grid=...]
    reshape x3 -> x1, local copies, waits for them, and re-layouts: 23.5 us -> 0.07 us  [body(): partial_value = jnp.sum(sums.reshape(-1, KC), axis=0)]
    sub x2 -> x0, local copies, waits for them, and re-layouts: 16.4 us -> none  [edge_flux(): return harmonic_mean(low_cond, high_cond) * (high_volt - low_volt)]
    dynamic_update_slice x8 -> x0, other arithmetic: 10.7 us -> none  [body(): diode_part = lax.map(diode_rows, (volt_field, diode_field))]
    dynamic_slice x8 -> x0, local copies, waits for them, and re-layouts: 10.3 us -> none  [body(): diode_part = lax.map(diode_rows, (volt_field, diode_field))]
  transfers between devices with their start and end apart: 4 -> 4, of which waited for: 0 -> 0; matrix products, arithmetic and copies ran while one was open for 56% -> 7% of each run, Pallas kernels for 0% -> 27%
where the time goes in v1:
time: 93.5 us; the launch traced here: 93 us
  blocking collectives  38.9 us (42%)
  Pallas kernels  31.1 us (33%)
  starting transfers between devices  10.7 us (11%)
  local copies, waits for them, and re-layouts  7.65 us (8%)
  other arithmetic  3.74 us (4%)
    psum x1, blocking collectives, body(): summed = lax.psum(partial_value, ('gx', 'gy'))  38.9 us
    pallas_call x1, Pallas kernels, body(): pl.pallas_call(functools.partial(main_kernel, regions, rows, cols), grid=...  25.3 us
    pallas_call x1, Pallas kernels, body(): pl.pallas_call(functools.partial(edge_kernel, rows - 1, width), grid=(2,...  5.78 us
    ppermute x2, starting transfers between devices, shift(): lax.ppermute(bottom, axis, backward)  5.76 us
    ppermute x2, starting transfers between devices, shift(): lax.ppermute(top, axis, forward)  4.95 us
  transfers between devices with their start and end apart: 4, of which 0 were waited for; matrix products, arithmetic and copies ran while one was open for 7% of the time, Pallas kernels for 27%

profile of v1, /device:TPU:0, one launch (start us, length us, event | category | flops | bytes accessed | tf_op | source)
XLA Modules:
  0.0 93.0 jit_solution(6635496851474299560)
XLA Ops:
  0.6 0.0 copy-start.3
  0.6 0.0 copy-start.4
  0.7 0.0 copy-start.5
  0.7 0.0 copy-start.1
  0.7 1.4 %fusion.3 = (f32[8,1,2048]{2,1,0:T(1,128)S(1)}, f32[8,1,2048]{2,1,0:T(1,128)S(1)}) fusion(f32[8,64,2048]{2,1,0:T(8,128)} %volt_ref.1), kind=kLoop, calls=%fused_computation.22 | loop fusion | bytes 262144 | tf_op jit(solution)/shard_map/slice | solution.py:251
  2.0 1.1 %fusion.4 = (s32[8,1,32]{1,2,0:T(8,128)S(1)}, s32[8,1,32]{1,2,0:T(8,128)S(1)}) fusion(s32[8,64,32]{1,2,0:T(8,128)} %param.10), kind=kLoop, calls=%fused_computation.23 | loop fusion | bytes 4096 | tf_op jit(solution)/shard_map/slice | solution.py:250
  3.1 0.1 copy.30
  3.2 0.1 copy.31
  3.4 0.8 select_reduce_fusion.3
  4.1 0.7 fusion
  4.8 4.9 %collective-permute-start = (f32[8,1,2176]{2,1,0:T(1,128)}, f32[8,1,2176]{2,1,0:T(1,128)S(1)}, u32[]{:S(2)}, u32[]{:S(2)}) collective-permute-start(f32[8,1,2176]{2,1,0:T(1,128)} %fusion), channel_id=1, source_target_pairs={{0,1},{2,3},{4,5},{6,7},{8,9},{10,11},{12,13},{14,15},{16,17},{18,... | collective-permute-start | bytes 208904 | tf_op jit(solution)/shard_map/ppermute | solution.py:231
  9.7 0.7 fusion.1
  10.4 1.3 %collective-permute-start.1 = (f32[8,1,2176]{2,1,0:T(1,128)}, f32[8,1,2176]{2,1,0:T(1,128)S(1)}, u32[]{:S(2)}, u32[]{:S(2)}) collective-permute-start(f32[8,1,2176]{2,1,0:T(1,128)} %fusion.1), channel_id=1, source_target_pairs={{1,0},{3,2},{5,4},{7,6},{9,8},{11,10},{13,12},{15,14},{17,16},{19,... | collective-permute-start | bytes 208904 | tf_op jit(solution)/shard_map/ppermute | solution.py:232
  11.7 0.7 slice_bitcast_fusion
  12.4 1.3 %fusion.2 = (f32[1,64,2048]{2,1,0:T(8,128)S(1)}, f32[1,64,2048]{2,1,0:T(8,128)S(1)}) fusion(f32[8,64,2048]{2,1,0:T(8,128)} %volt_ref.1), kind=kLoop, calls=%fused_computation.21 | loop fusion | bytes 2097152 | tf_op jit(solution)/shard_map/slice | solution.py:253
  13.7 0.8 select_reduce_fusion.1
  14.5 0.1 copy.28
  14.7 0.1 collective-permute-start.2
  14.7 0.1 copy.29
  14.9 4.5 %collective-permute-start.3 = (f32[1,64,2176]{2,1,0:T(8,128)S(1)}, f32[1,64,2176]{2,1,0:T(8,128)S(1)}, u32[]{:S(2)}, u32[]{:S(2)}) collective-permute-start(f32[1,64,2176]{2,1,0:T(8,128)S(1)} %select_maximum_fusion), channel_id=1, source_target_pairs={{2,0},{4,2},{6,4},{8,6},{10,8},{12,10},{14,12},{16,14},{18,16},{20... | collective-permute-start | bytes 1671176 | tf_op jit(solution)/shard_map/ppermute | solution.py:232
  19.3 0.1 copy.25.region_ref
  19.5 0.2 select_reduce_fusion
  19.7 0.7 copy.27
  20.4 1.0 %copy.26.mask_ref = s32[8,64,32]{2,1,0:T(8,128)S(1)} copy(s32[8,64,32]{1,2,0:T(8,128)} %param.11) | data formatting | bytes 131072 | tf_op args[3]
  21.4 0.8 pad.20.cond_ref
  22.3 0.0 collective-permute-done.left_ref
  22.3 25.3 %cells.1 = (f32[8,64,2048]{2,1,0:T(8,128)}, f32[8,128]{1,0:T(8,128)S(1)}) custom-call(f32[8,64,2048]{2,1,0:T(8,128)} %volt_ref.1, f32[8,64,2048]{2,1,0:T(8,128)} %drive_ref.1, s32[8,64,32]{2,1,0:T(8,128)S(1)} %copy.25.region_ref, s32[8,64,32]{2,1,0:T(8,128)S(1)} %copy.26.mask_ref, f32[8,1,2176]{2,1,0:T(1,128)S(1)} %collective-permute-done.left_ref, ...), custom_call_target="tpu_custom_call" | custom-call | flops 20000000000 | bytes 12582912 | tf_op jit(solution)/shard_map/cells/pallas_call | solution.py:259
  47.6 0.0 collective-permute-done.2.low_ref
  47.6 5.8 %edges.1 = (f32[8,64,2048]{2,1,0:T(8,128)}, f32[8,128]{1,0:T(8,128)S(1)}) custom-call(f32[8,64,2048]{2,1,0:T(8,128)} %get-tuple-element.6.part_ref, f32[8,64,2048]{2,1,0:T(8,128)S(1)} %copy-done, f32[2,64,128]{2,1,0:T(8,128)S(1)} %pad.20.cond_ref, f32[1,64,2176]{2,1,0:T(8,128)S(1)} %collective-permute-done.2.low_ref, ...), custom_call_target="tpu_custom_call", output_to_operand_aliasing={{0}: (0, {})} | custom-call | tf_op jit(solution)/shard_map/edges/pallas_call | solution.py:300
  53.4 0.1 reshape.72
  53.5 38.9 %psum.7 = f32[64]{0:T(128)S(1)} all-reduce(f32[64]{0:T(128)S(1)} %reduce_sum.71), channel_id=1, replica_groups=mesh['gx'=16,'gy'=2] {'gx','gy'}, use_global_device_ids=true, to_apply=%region_6.7 | all-reduce | flops 64 | bytes 512 | tf_op jit(solution)/shard_map/psum | solution.py:333
  92.5 0.5 add_sqrt_fusion
  (14 shorter events, 0.1 us)
Async XLA Ops:
  0.6 21.6 %copy-start.3 = (bf16[1024,256]{1,0:T(8,128)(2,1)S(1)}, bf16[1024,256]{1,0:T(8,128)(2,1)}, u32[]{:S(2)}) copy-start(bf16[1024,256]{1,0:T(8,128)(2,1)} %constant.14.clone.back_ref) | copy-start | bytes 1572868
  0.6 21.6 %copy-start.4 = (bf16[256,256]{1,0:T(8,128)(2,1)S(1)}, bf16[256,256]{1,0:T(8,128)(2,1)}, u32[]{:S(2)}) copy-start(bf16[256,256]{1,0:T(8,128)(2,1)} %constant.13.clone.forward_ref) | copy-start | bytes 393220
  0.7 18.7 %copy-start.5 = (s32[8,64,32]{1,2,0:T(8,128)S(1)}, s32[8,64,32]{1,2,0:T(8,128)}, u32[]{:S(2)}) copy-start(s32[8,64,32]{1,2,0:T(8,128)} %param.10) | copy-start | bytes 196612
  0.7 18.8 %copy-start.1 = (f32[8]{0:T(128)S(1)}, f32[8]{0:T(128)}, u32[]{:S(2)}) copy-start(f32[8]{0:T(128)} %sigma_ref.1) | copy-start | bytes 100
  0.7 21.6 %copy-start.2 = (f32[8]{0:T(128)S(1)}, f32[8]{0:T(128)}, u32[]{:S(2)}) copy-start(f32[8]{0:T(128)} %cap_ref.1) | copy-start | bytes 100
  4.8 17.4 %collective-permute-start = (f32[8,1,2176]{2,1,0:T(1,128)}, f32[8,1,2176]{2,1,0:T(1,128)S(1)}, u32[]{:S(2)}, u32[]{:S(2)}) collective-permute-start(f32[8,1,2176]{2,1,0:T(1,128)} %fusion), channel_id=1, source_target_pairs={{0,1},{2,3},{4,5},{6,7},{8,9},{10,11},{12,13},{14,15},{16,17},{18,... | collective-permute-start | bytes 208904 | tf_op jit(solution)/shard_map/ppermute | solution.py:231
  10.4 11.9 %collective-permute-start.1 = (f32[8,1,2176]{2,1,0:T(1,128)}, f32[8,1,2176]{2,1,0:T(1,128)S(1)}, u32[]{:S(2)}, u32[]{:S(2)}) collective-permute-start(f32[8,1,2176]{2,1,0:T(1,128)} %fusion.1), channel_id=1, source_target_pairs={{1,0},{3,2},{5,4},{7,6},{9,8},{11,10},{13,12},{15,14},{17,16},{19,... | collective-permute-start | bytes 208904 | tf_op jit(solution)/shard_map/ppermute | solution.py:232
  14.7 33.0 %collective-permute-start.2 = (f32[1,64,2176]{2,1,0:T(8,128)S(1)}, f32[1,64,2176]{2,1,0:T(8,128)S(1)}, u32[]{:S(2)}, u32[]{:S(2)}) collective-permute-start(f32[1,64,2176]{2,1,0:T(8,128)S(1)} %select_maximum_fusion.1), channel_id=1, source_target_pairs={{0,2},{2,4},{4,6},{6,8},{8,10},{10,12},{12,14},{14,16},{16,18},{18... | collective-permute-start | bytes 1671176 | tf_op jit(solution)/shard_map/ppermute | solution.py:231
  14.9 32.8 %collective-permute-start.3 = (f32[1,64,2176]{2,1,0:T(8,128)S(1)}, f32[1,64,2176]{2,1,0:T(8,128)S(1)}, u32[]{:S(2)}, u32[]{:S(2)}) collective-permute-start(f32[1,64,2176]{2,1,0:T(8,128)S(1)} %select_maximum_fusion), channel_id=1, source_target_pairs={{2,0},{4,2},{6,4},{8,6},{10,8},{12,10},{14,12},{16,14},{18,16},{20... | collective-permute-start | bytes 1671176 | tf_op jit(solution)/shard_map/ppermute | solution.py:232
  22.2 25.4 %copy-start = (f32[8,64,2048]{2,1,0:T(8,128)S(1)}, f32[8,64,2048]{2,1,0:T(8,128)}, u32[]{:S(2)}) copy-start(f32[8,64,2048]{2,1,0:T(8,128)} %volt_ref.1) | copy-start | bytes 12582916

commit v2 on v1

--- a/solution.py
+++ b/solution.py
@@ -221,6 +221,55 @@
     sum_ref[...] = acc_ref[...]
 
 
+def exchange(axis, count, here, got_ref, send, recv):
+    def copy(peer, slot):
+        return pltpu.make_async_remote_copy(
+            src_ref=got_ref.at[here],
+            dst_ref=got_ref.at[slot],
+            send_sem=send.at[peer],
+            recv_sem=recv.at[slot],
+            device_id={axis: peer},
+            device_id_type=pl.DeviceIdType.MESH,
+        )
+
+    peers = [lax.rem(here + d, count) for d in range(1, count)]
+    for peer in peers:
+        copy(peer, here).start()
+    for peer in peers:
+        copy(peer, peer).wait_recv()
+    for peer in peers:
+        copy(peer, here).wait_send()
+
+
+def greet(axis, count, here):
+    barrier = pltpu.get_barrier_semaphore()
+    for d in range(1, count):
+        pl.semaphore_signal(
+            barrier,
+            inc=1,
+            device_id={axis: lax.rem(here + d, count)},
+            device_id_type=pl.DeviceIdType.MESH,
+        )
+
+
+def norm_of(total, cells):
+    value = jnp.broadcast_to(jnp.sum(total, axis=0, keepdims=True), total.shape)
+    value = value + pltpu.roll(value, KC, 1)
+    return jnp.sqrt(value / cells + norm_eps)
+
+
+def reduce_kernel(nx, ny, cells, in_ref, out_ref, got_x, got_y, send_x, recv_x, send_y, recv_y):
+    me_x, me_y = lax.axis_index("gx"), lax.axis_index("gy")
+    greet("gx", nx, me_x)
+    greet("gy", ny, me_y)
+    got_x[me_x] = in_ref[...]
+    pl.semaphore_wait(pltpu.get_barrier_semaphore(), nx + ny - 2)
+    exchange("gx", nx, me_x, got_x, send_x, recv_x)
+    got_y[me_y] = jnp.sum(got_x[...], axis=0)
+    exchange("gy", ny, me_y, got_y, send_y, recv_y)
+    out_ref[...] = norm_of(jnp.sum(got_y[...], axis=0), cells)
+
+
 def shift(block, axis, periodic):
     count = lax.axis_size(axis)
     forward = [(k, k + 1) for k in range(count - 1)]
@@ -329,10 +378,24 @@
         name="edges",
     )(part, volt, conduct_of(ends), low, high, squares)
 
-    partial_value = jnp.sum(sums.reshape(-1, KC), axis=0)
-    summed = lax.psum(partial_value, ("gx", "gy"))
-    cells_total = rows * cols * NZ * lax.axis_size("gx") * lax.axis_size("gy")
-    return residual, jnp.sqrt(summed / cells_total + norm_eps)
+    nx, ny = lax.axis_size("gx"), lax.axis_size("gy")
+    norms = pl.pallas_call(
+        functools.partial(reduce_kernel, nx, ny, float(rows * cols * NZ * nx * ny)),
+        out_shape=jax.ShapeDtypeStruct((8, LANES), jnp.float32),
+        in_specs=[pl.BlockSpec(memory_space=pltpu.VMEM)],
+        out_specs=pl.BlockSpec(memory_space=pltpu.VMEM),
+        scratch_shapes=[
+            pltpu.VMEM((nx, 8, LANES), jnp.float32),
+            pltpu.VMEM((ny, 8, LANES), jnp.float32),
+            pltpu.SemaphoreType.DMA((nx,)),
+            pltpu.SemaphoreType.DMA((nx,)),
+            pltpu.SemaphoreType.DMA((ny,)),
+            pltpu.SemaphoreType.DMA((ny,)),
+        ],
+        compiler_params=pltpu.CompilerParams(collective_id=0, has_side_effects=True),
+        name="norms",
+    )(sums)
+    return residual, norms[0, :KC]
 
 
 def solution(mesh):

time: 93.5 us -> 68 us (0.73)
  blocking collectives: 38.9 us -> 0 us
  Pallas kernels: 31.1 us -> 43.3 us
  local copies, waits for them, and re-layouts: 7.65 us -> 9.37 us
    psum x1 -> x0, blocking collectives: 38.9 us -> none  [body(): summed = lax.psum(partial_value, ('gx', 'gy'))]
    pallas_call x0 -> x1, Pallas kernels: none -> 12.3 us  [body(): pl.pallas_call(functools.partial(reduce_kernel, nx, ny, float(rows * cols...]
    squeeze x0 -> x1, local copies, waits for them, and re-layouts: none -> 1.2 us  [body(): return (residual, norms[0, :KC])]
    unnamed x16 -> x18, local copies, waits for them, and re-layouts: 1.43 us -> 2.02 us
  transfers between devices with their start and end apart: 4 -> 4, of which waited for: 0 -> 0; matrix products, arithmetic and copies ran while one was open for 7% -> 10% of each run, Pallas kernels for 27% -> 37%
where the time goes in v2:
time: 68 us; the launch traced here: 67.5 us
  Pallas kernels  43.3 us (64%)
  starting transfers between devices  10.7 us (16%)
  local copies, waits for them, and re-layouts  9.37 us (14%)
  other arithmetic  3.19 us (5%)
  between operations  0.86 us (1%)
    pallas_call x1, Pallas kernels, body(): pl.pallas_call(functools.partial(main_kernel, regions, rows, cols), grid=...  25.3 us
    pallas_call x1, Pallas kernels, body(): pl.pallas_call(functools.partial(reduce_kernel, nx, ny, float(rows * cols...  12.3 us
    pallas_call x1, Pallas kernels, body(): pl.pallas_call(functools.partial(edge_kernel, rows - 1, width), grid=(2,...  5.78 us
    ppermute x2, starting transfers between devices, shift(): lax.ppermute(bottom, axis, backward)  5.76 us
    ppermute x2, starting transfers between devices, shift(): lax.ppermute(top, axis, forward)  4.95 us
    unnamed x18, local copies, waits for them, and re-layouts  2.02 us
    reduce_sum x3, other arithmetic, conduct_of(): value = jnp.sum(jnp.where(onehot, sigma_table, 0.0), axis=-1)  1.73 us
    concatenate x4, other arithmetic, packed(): return jnp.concatenate([volt_part, conduct_of(region_part)], axis=-1)  1.46 us
  transfers between devices with their start and end apart: 4, of which 0 were waited for; matrix products, arithmetic and copies ran while one was open for 10% of the time, Pallas kernels for 37%

profile of v2, /device:TPU:0, one launch (start us, length us, event | category | flops | bytes accessed | tf_op | source)
XLA Modules:
  0.0 67.5 jit_solution(6389144544256588381)
XLA Ops:
  0.6 0.0 copy-start.4
  0.6 0.0 copy-start.5
  0.7 0.0 copy-start.6
  0.7 0.0 copy-start.1
  0.7 1.4 %fusion.3 = (f32[8,1,2048]{2,1,0:T(1,128)S(1)}, f32[8,1,2048]{2,1,0:T(1,128)S(1)}) fusion(f32[8,64,2048]{2,1,0:T(8,128)} %volt_ref.1), kind=kLoop, calls=%fused_computation.22 | loop fusion | bytes 262144 | tf_op jit(solution)/shard_map/slice | solution.py:300
  2.0 1.1 %fusion.4 = (s32[8,1,32]{1,2,0:T(8,128)S(1)}, s32[8,1,32]{1,2,0:T(8,128)S(1)}) fusion(s32[8,64,32]{1,2,0:T(8,128)} %param.10), kind=kLoop, calls=%fused_computation.23 | loop fusion | bytes 4096 | tf_op jit(solution)/shard_map/slice | solution.py:299
  3.1 0.1 copy.30
  3.2 0.1 copy.31
  3.4 0.8 %select_reduce_fusion.3 = (f32[8,32]{1,0:T(8,128)S(1)}, f32[8,32]{1,0:T(8,128)S(1)}) fusion(s32[8,32]{1,0:T(8,128)S(1)} %bitcast.17, f32[8]{0:T(128)} %sigma_ref.1, s32[8,32]{1,0:T(8,128)S(1)} %bitcast.15), kind=kLoop, calls=%fused_computation.14 | loop fusion | flops 11776 | bytes 4128 | tf_op jit(solution)/shard_map/reduce_sum | solution.py:291
  4.1 0.7 %fusion = f32[8,1,2176]{2,1,0:T(1,128)} fusion(f32[8,1,32]{2,1,0:T(1,128)S(1)} %bitcast.16, f32[8,1,2048]{2,1,0:T(1,128)S(1)} %get-tuple-element.17), kind=kLoop, calls=%fused_computation.11 | loop fusion | flops 52224 | bytes 136192 | tf_op jit(solution)/shard_map/concatenate | solution.py:295
  4.8 4.9 %collective-permute-start = (f32[8,1,2176]{2,1,0:T(1,128)}, f32[8,1,2176]{2,1,0:T(1,128)S(1)}, u32[]{:S(2)}, u32[]{:S(2)}) collective-permute-start(f32[8,1,2176]{2,1,0:T(1,128)} %fusion), channel_id=1, source_target_pairs={{0,1},{2,3},{4,5},{6,7},{8,9},{10,11},{12,13},{14,15},{16,17},{18,... | collective-permute-start | bytes 208904 | tf_op jit(solution)/shard_map/ppermute | solution.py:280
  9.7 0.7 %fusion.1 = f32[8,1,2176]{2,1,0:T(1,128)} fusion(f32[8,1,32]{2,1,0:T(1,128)S(1)} %bitcast.14, f32[8,1,2048]{2,1,0:T(1,128)S(1)} %get-tuple-element.16), kind=kLoop, calls=%fused_computation.12 | loop fusion | flops 52224 | bytes 136192 | tf_op jit(solution)/shard_map/concatenate | solution.py:295
  10.4 1.3 %collective-permute-start.1 = (f32[8,1,2176]{2,1,0:T(1,128)}, f32[8,1,2176]{2,1,0:T(1,128)S(1)}, u32[]{:S(2)}, u32[]{:S(2)}) collective-permute-start(f32[8,1,2176]{2,1,0:T(1,128)} %fusion.1), channel_id=1, source_target_pairs={{1,0},{3,2},{5,4},{7,6},{9,8},{11,10},{13,12},{15,14},{17,16},{19,... | collective-permute-start | bytes 208904 | tf_op jit(solution)/shard_map/ppermute | solution.py:281
  11.7 0.7 %slice_bitcast_fusion.1 = (s32[64,32]{0,1:T(8,128)S(1)}, s32[64,32]{0,1:T(8,128)S(1)}, s32[1,64,32]{1,2,0:T(8,128)S(1)}, s32[1,64,32]{1,2,0:T(8,128)S(1)}) fusion(s32[8,64,32]{1,2,0:T(8,128)} %param.10), kind=kLoop, calls=%fused_computation.19 | loop fusion | bytes 49152 | tf_op jit(solution)/shard_map/eq | solution.py:290
  12.4 1.3 %fusion.2 = (f32[1,64,2048]{2,1,0:T(8,128)S(1)}, f32[1,64,2048]{2,1,0:T(8,128)S(1)}) fusion(f32[8,64,2048]{2,1,0:T(8,128)} %volt_ref.1), kind=kLoop, calls=%fused_computation.21 | loop fusion | bytes 2097152 | tf_op jit(solution)/shard_map/slice | solution.py:302
  13.7 0.8 %select_reduce_fusion.1 = (f32[64,32]{0,1:T(8,128)S(1)}, f32[64,32]{0,1:T(8,128)S(1)}) fusion(s32[64,32]{0,1:T(8,128)S(1)} %get-tuple-element.19, f32[8]{0:T(128)} %sigma_ref.1, s32[64,32]{0,1:T(8,128)S(1)} %get-tuple-element.18), kind=kLoop, calls=%fused_computation.7 | loop fusion | flops 94208 | bytes 32800 | tf_op jit(solution)/shard_map/reduce_sum | solution.py:291
  14.5 0.1 copy.28
  14.7 0.1 collective-permute-start.2
  14.7 0.1 copy.29
  14.9 4.5 %collective-permute-start.3 = (f32[1,64,2176]{2,1,0:T(8,128)S(1)}, f32[1,64,2176]{2,1,0:T(8,128)S(1)}, u32[]{:S(2)}, u32[]{:S(2)}) collective-permute-start(f32[1,64,2176]{2,1,0:T(8,128)S(1)} %select_maximum_fusion), channel_id=1, source_target_pairs={{2,0},{4,2},{6,4},{8,6},{10,8},{12,10},{14,12},{16,14},{18,16},{20... | collective-permute-start | bytes 1671176 | tf_op jit(solution)/shard_map/ppermute | solution.py:281
  19.3 0.1 copy.25.region_ref
  19.5 0.2 select_reduce_fusion
  19.7 0.7 %copy.27 = f32[2,64,32]{2,1,0:T(8,128)} copy(f32[2,64,32]{1,2,0:T(8,128)S(1)} %select_reduce_fusion) | data formatting | bytes 32768 | tf_op jit(solution)/shard_map/reduce_sum | solution.py:291
  20.4 1.0 %copy.26.mask_ref = s32[8,64,32]{2,1,0:T(8,128)S(1)} copy(s32[8,64,32]{1,2,0:T(8,128)} %param.11) | data formatting | bytes 131072 | tf_op args[3]
  21.4 0.8 %pad.20.cond_ref = f32[2,64,128]{2,1,0:T(8,128)S(1)} pad(f32[2,64,32]{2,1,0:T(8,128)} %copy.27, f32[]{:T(128)} %constant.3.clone.1), padding=0_0x0_0x0_96 | pad | bytes 81924 | tf_op jit(solution)/shard_map/jit(_pad)/pad | solution.py:292
  22.2 0.0 collective-permute-done.left_ref
  22.3 0.0 collective-permute-done.1.right_ref
  22.3 25.3 %cells.1 = (f32[8,64,2048]{2,1,0:T(8,128)}, f32[8,128]{1,0:T(8,128)S(1)}) custom-call(f32[8,64,2048]{2,1,0:T(8,128)} %volt_ref.1, f32[8,64,2048]{2,1,0:T(8,128)} %drive_ref.1, s32[8,64,32]{2,1,0:T(8,128)S(1)} %copy.25.region_ref, s32[8,64,32]{2,1,0:T(8,128)S(1)} %copy.26.mask_ref, f32[8,1,2176]{2,1,0:T(1,128)S(1)} %collective-permute-done.left_ref, ...), custom_call_target="tpu_custom_call" | custom-call | flops 20000000000 | bytes 12582912 | tf_op jit(solution)/shard_map/cells/pallas_call | solution.py:308
  47.6 5.8 %edges.1 = (f32[8,64,2048]{2,1,0:T(8,128)}, f32[8,128]{1,0:T(8,128)S(1)}) custom-call(f32[8,64,2048]{2,1,0:T(8,128)} %get-tuple-element.6.part_ref, f32[8,64,2048]{2,1,0:T(8,128)S(1)} %copy-done, f32[2,64,128]{2,1,0:T(8,128)S(1)} %pad.20.cond_ref, f32[1,64,2176]{2,1,0:T(8,128)S(1)} %collective-permute-done.2.low_ref, ...), custom_call_target="tpu_custom_call", output_to_operand_aliasing={{0}: (0, {})} | custom-call | tf_op jit(solution)/shard_map/edges/pallas_call | solution.py:349
  53.4 0.6 copy-done.2
  54.0 12.3 %norms.1 = f32[8,128]{1,0:T(8,128)} custom-call(f32[8,128]{1,0:T(8,128)} %copy-done.2), custom_call_target="tpu_custom_call" | custom-call | tf_op jit(solution)/shard_map/norms/pallas_call | solution.py:382
  66.3 1.2 %slice_bitcast_fusion = f32[64]{0:T(128)} fusion(f32[8,128]{1,0:T(8,128)} %norms.1), kind=kLoop, calls=%fused_computation.18 | loop fusion | bytes 512 | tf_op jit(solution)/shard_map/squeeze | solution.py:398
  (14 shorter events, 0.1 us)
Async XLA Ops:
  0.6 21.6 %copy-start.4 = (bf16[1024,256]{1,0:T(8,128)(2,1)S(1)}, bf16[1024,256]{1,0:T(8,128)(2,1)}, u32[]{:S(2)}) copy-start(bf16[1024,256]{1,0:T(8,128)(2,1)} %constant.9.clone.back_ref) | copy-start | bytes 1572868
  0.6 21.6 %copy-start.5 = (bf16[256,256]{1,0:T(8,128)(2,1)S(1)}, bf16[256,256]{1,0:T(8,128)(2,1)}, u32[]{:S(2)}) copy-start(bf16[256,256]{1,0:T(8,128)(2,1)} %constant.8.clone.forward_ref) | copy-start | bytes 393220
  0.7 18.7 %copy-start.6 = (s32[8,64,32]{1,2,0:T(8,128)S(1)}, s32[8,64,32]{1,2,0:T(8,128)}, u32[]{:S(2)}) copy-start(s32[8,64,32]{1,2,0:T(8,128)} %param.10) | copy-start | bytes 196612
  0.7 18.8 %copy-start.1 = (f32[8]{0:T(128)S(1)}, f32[8]{0:T(128)}, u32[]{:S(2)}) copy-start(f32[8]{0:T(128)} %sigma_ref.1) | copy-start | bytes 100
  0.7 21.6 %copy-start.3 = (f32[8]{0:T(128)S(1)}, f32[8]{0:T(128)}, u32[]{:S(2)}) copy-start(f32[8]{0:T(128)} %cap_ref.1) | copy-start | bytes 100
  4.8 17.4 %collective-permute-start = (f32[8,1,2176]{2,1,0:T(1,128)}, f32[8,1,2176]{2,1,0:T(1,128)S(1)}, u32[]{:S(2)}, u32[]{:S(2)}) collective-permute-start(f32[8,1,2176]{2,1,0:T(1,128)} %fusion), channel_id=1, source_target_pairs={{0,1},{2,3},{4,5},{6,7},{8,9},{10,11},{12,13},{14,15},{16,17},{18,... | collective-permute-start | bytes 208904 | tf_op jit(solution)/shard_map/ppermute | solution.py:280
  10.4 11.9 %collective-permute-start.1 = (f32[8,1,2176]{2,1,0:T(1,128)}, f32[8,1,2176]{2,1,0:T(1,128)S(1)}, u32[]{:S(2)}, u32[]{:S(2)}) collective-permute-start(f32[8,1,2176]{2,1,0:T(1,128)} %fusion.1), channel_id=1, source_target_pairs={{1,0},{3,2},{5,4},{7,6},{9,8},{11,10},{13,12},{15,14},{17,16},{19,... | collective-permute-start | bytes 208904 | tf_op jit(solution)/shard_map/ppermute | solution.py:281
  14.7 33.0 %collective-permute-start.2 = (f32[1,64,2176]{2,1,0:T(8,128)S(1)}, f32[1,64,2176]{2,1,0:T(8,128)S(1)}, u32[]{:S(2)}, u32[]{:S(2)}) collective-permute-start(f32[1,64,2176]{2,1,0:T(8,128)S(1)} %select_maximum_fusion.1), channel_id=1, source_target_pairs={{0,2},{2,4},{4,6},{6,8},{8,10},{10,12},{12,14},{14,16},{16,18},{18... | collective-permute-start | bytes 1671176 | tf_op jit(solution)/shard_map/ppermute | solution.py:280
  14.9 32.8 %collective-permute-start.3 = (f32[1,64,2176]{2,1,0:T(8,128)S(1)}, f32[1,64,2176]{2,1,0:T(8,128)S(1)}, u32[]{:S(2)}, u32[]{:S(2)}) collective-permute-start(f32[1,64,2176]{2,1,0:T(8,128)S(1)} %select_maximum_fusion), channel_id=1, source_target_pairs={{2,0},{4,2},{6,4},{8,6},{10,8},{12,10},{14,12},{16,14},{18,16},{20... | collective-permute-start | bytes 1671176 | tf_op jit(solution)/shard_map/ppermute | solution.py:281
  22.2 25.4 %copy-start = (f32[8,64,2048]{2,1,0:T(8,128)S(1)}, f32[8,64,2048]{2,1,0:T(8,128)}, u32[]{:S(2)}) copy-start(f32[8,64,2048]{2,1,0:T(8,128)} %volt_ref.1) | copy-start | bytes 12582916
  53.4 0.6 copy-start.2

commit v3 on v2

v3 whole, which is shorter than its diff:
```python
import functools
import math

import jax
import jax.numpy as jnp
import numpy as np
from jax import lax
from jax.experimental import pallas as pl
from jax.experimental.pallas import tpu as pltpu
from jax.sharding import PartitionSpec as P

NZ = 32
H = 32
KC = 64
S = 256
LANES = 128
TILES = NZ * KC // LANES
CHUNK = 8
BLOCK = 8

base_freq = 0.1
norm_eps = 1e-06


def tables():
    orders = np.arange(1, H + 1, dtype=np.float64)
    angles = orders[:, None] * (2.0 * math.pi * np.arange(S) / S)[None, :]
    synthesis = np.concatenate([np.cos(angles), np.sin(angles)], axis=0)
    analysis = synthesis.T * (2.0 / S)
    derived = np.concatenate(
        [base_freq * orders * analysis[:, H:], -base_freq * orders * analysis[:, :H]], axis=1
    )

    def split(table):
        high = table.astype(jnp.bfloat16)
        low = (table - high.astype(np.float64)).astype(jnp.bfloat16)
        return high, low

    high, low = split(synthesis)
    forward = np.concatenate([high, high, low, low], axis=0)
    cell = 0.5 * np.concatenate([analysis, derived], axis=0)
    both = np.zeros((4 * S, LANES))
    both[: 2 * S, :KC] = cell
    both[2 * S :, KC:] = cell
    high, low = split(both)
    return jnp.asarray(forward), jnp.asarray(np.concatenate([high, low], axis=1))


def lookup(region, table, count):
    value = jnp.where(region == 0, table[0], 0.0)
    for r in range(1, count):
        value = jnp.where(region == r, table[r], value)
    return value


def harmonic_mean(left, right):
    return 2.0 * left * right / (left + right)


def spread(cells, tile, lane, base=0):
    index = base + 2 * tile + (lane >= KC).astype(jnp.int32)
    return jnp.take_along_axis(cells, index, axis=1, mode="promise_in_bounds")


def main_kernel(
    rows, cols,
    volt_hbm, low_hbm, high_hbm, drive_ref, cells_ref, low_cells, high_cells,
    left_ref, right_ref, left_cells, right_cells, forward_ref, back_ref,
    out_ref, squares_ref, volt_buf, acc_ref, sems,
):
    i = pl.program_id(0)
    sources = [low_hbm] + [volt_hbm.at[row] for row in range(rows)] + [high_hbm]

    def copy(slot):
        return pltpu.make_async_copy(sources[slot], volt_buf.at[slot], sems.at[slot])

    @pl.when(i == 0)
    def _():
        for slot in range(rows + 2):
            copy(slot).start()
        acc_ref[...] = jnp.zeros_like(acc_ref)
        copy(0).wait()
        copy(1).wait()

    for slot in range(2, rows + 2):

        @pl.when(i == slot - 2)
        def _():
            copy(slot).wait()

    lane = lax.broadcasted_iota(jnp.int32, (cols, LANES), 1)
    col = lax.broadcasted_iota(jnp.int32, (cols, LANES), 0)
    cells = cells_ref[i]
    prev_cells = jnp.where(i > 0, cells_ref[jnp.maximum(i - 1, 0)], low_cells[...])
    next_cells = jnp.where(
        i < rows - 1, cells_ref[jnp.minimum(i + 1, rows - 1)], high_cells[...]
    )
    me, count = lax.axis_index("gy"), lax.axis_size("gy")
    has_left, has_right = me > 0, me < count - 1
    g_low = harmonic_mean(cells, prev_cells)
    g_high = harmonic_mean(cells, next_cells)
    edge_left = jnp.where(has_left, left_cells[0, BLOCK - 1 :, :], 0.0)
    edge_right = jnp.where(has_right, right_cells[0, :1, :], 0.0)
    cells_after = jnp.where(
        col == cols - 1, jnp.broadcast_to(edge_right, cells.shape), pltpu.roll(cells, cols - 1, 0)
    )
    g_col = harmonic_mean(cells, cells_after)
    g_left = harmonic_mean(cells[:8], jnp.broadcast_to(edge_left, (8, LANES)))
    g_depth = jnp.where(
        lane < NZ - 1, harmonic_mean(cells, pltpu.roll(cells, LANES - 1, 1)), 0.0
    )

    first = lane < KC
    half = lane % KC
    order = base_freq * (half % H + 1).astype(jnp.float32)
    order = jnp.where(half < H, order, -order)
    swap = lane ^ H

    prev_flux = None
    total = jnp.zeros((8, LANES), jnp.float32)
    for start in range(0, TILES, CHUNK):
        xa, xb, turned = [], [], []
        for t in range(start, start + CHUNK):
            v = volt_buf[i + 1, :, t * LANES : (t + 1) * LANES]
            high = v.astype(jnp.bfloat16).astype(jnp.float32)
            low = v - high
            high_r = pltpu.roll(high, KC, 1)
            low_r = pltpu.roll(low, KC, 1)
            xa.append(jnp.where(first, high, low_r).astype(jnp.bfloat16))
            xb.append(jnp.where(first, high_r, low).astype(jnp.bfloat16))
            turned.append(high_r + low_r)
        if start + CHUNK < TILES:
            t = start + CHUNK
            turned.append(pltpu.roll(volt_buf[i + 1, :, t * LANES : (t + 1) * LANES], KC, 1))
        else:
            turned.append(turned[-1])
        x = jnp.concatenate(xa + xb, axis=0)
        samples = jnp.dot(
            jnp.concatenate([x, x], axis=1), forward_ref[...], preferred_element_type=jnp.float32
        )
        size = jnp.abs(samples)
        small = jnp.exp2(size * (-2.0 / math.log(2.0)) - 1.0)
        even = (size + jnp.log(0.5 + small)).astype(jnp.bfloat16)
        charge = jnp.tanh(samples.astype(jnp.bfloat16))
        m = CHUNK * cols
        waves = jnp.concatenate([even[:m], charge[:m], even[m:], charge[m:]], axis=1)
        projected = jnp.dot(waves, back_ref[...], preferred_element_type=jnp.float32)
        projected = projected[:, :LANES] + projected[:, LANES:]
        for t in range(start, start + CHUNK):
            at = slice(t * LANES, (t + 1) * LANES)
            v = volt_buf[i + 1, :, at]
            value = spread(g_low, t, lane) * (v - volt_buf[i, :, at])
            value -= spread(g_high, t, lane) * (volt_buf[i + 2, :, at] - v)
            right = jnp.where(has_right, right_ref[0, :1, at], 0.0)
            v_after = jnp.where(
                col == cols - 1, jnp.broadcast_to(right, v.shape), pltpu.roll(v, cols - 1, 0)
            )
            col_flux = spread(g_col, t, lane) * (v_after - v)
            left = jnp.where(has_left, left_ref[0, BLOCK - 1 :, at], 0.0)
            left_flux = spread(g_left, t, lane[:8]) * (v[:8] - jnp.broadcast_to(left, (8, LANES)))
            left_flux = jnp.concatenate([left_flux] * (cols // 8), axis=0)
            value += jnp.where(col == 0, left_flux, pltpu.roll(col_flux, 1, 0)) - col_flux
            v_deep = jnp.where(first, turned[t - start], turned[t - start + 1])
            deep_flux = spread(g_depth, t, lane) * (v_deep - v)
            deep_r = pltpu.roll(deep_flux, KC, 1)
            before = jnp.zeros_like(deep_r) if prev_flux is None else prev_flux
            value += jnp.where(first, before, deep_r) - deep_flux
            prev_flux = deep_r
            swapped = jnp.take_along_axis(v, swap, axis=1, mode="promise_in_bounds")
            value += spread(cells, t, lane, NZ) * (order * swapped)
            rows_of = slice((t - start) * cols, (t - start + 1) * cols)
            value += spread(cells, t, lane, 2 * NZ) * (projected[rows_of] + 0.5 * v)
            value -= drive_ref[0, :, at]
            out_ref[0, :, at] = value
            total += jnp.sum((value * value).reshape(cols // 8, 8, LANES), axis=0)
    acc_ref[...] += total

    @pl.when(i == rows - 1)
    def _():
        squares_ref[...] = acc_ref[...]


def exchange(axis, count, here, got_ref, send, recv):
    def copy(peer, slot):
        return pltpu.make_async_remote_copy(
            src_ref=got_ref.at[here],
            dst_ref=got_ref.at[slot],
            send_sem=send.at[peer],
            recv_sem=recv.at[slot],
            device_id={axis: peer},
            device_id_type=pl.DeviceIdType.MESH,
        )

    peers = [lax.rem(here + d, count) for d in range(1, count)]
    for peer in peers:
        copy(peer, here).start()
    for peer in peers:
        copy(peer, peer).wait_recv()
    for peer in peers:
        copy(peer, here).wait_send()


def greet(axis, count, here):
    barrier = pltpu.get_barrier_semaphore()
    for d in range(1, count):
        pl.semaphore_signal(
            barrier,
            inc=1,
            device_id={axis: lax.rem(here + d, count)},
            device_id_type=pl.DeviceIdType.MESH,
        )


def norm_of(total, cells):
    value = jnp.broadcast_to(jnp.sum(total, axis=0, keepdims=True), total.shape)
    value = value + pltpu.roll(value, KC, 1)
    return jnp.sqrt(value / cells + norm_eps)


def reduce_kernel(nx, ny, cells, in_ref, out_ref, got_x, got_y, send_x, recv_x, send_y, recv_y):
    me_x, me_y = lax.axis_index("gx"), lax.axis_index("gy")
    greet("gx", nx, me_x)
    greet("gy", ny, me_y)
    got_x[me_x] = in_ref[...]
    pl.semaphore_wait(pltpu.get_barrier_semaphore(), nx + ny - 2)
    exchange("gx", nx, me_x, got_x, send_x, recv_x)
    got_y[me_y] = jnp.sum(got_x[...], axis=0)
    exchange("gy", ny, me_y, got_y, send_y, recv_y)
    out_ref[...] = norm_of(jnp.sum(got_y[...], axis=0), cells)


def halo_kernel(
    nx, ny, rows, cols, volt, cells,
    low, low_cells, high, high_cells, left, left_cells, right, right_cells, send, recv,
):
    me_x, me_y = lax.axis_index("gx"), lax.axis_index("gy")
    up, down = lax.rem(me_x + 1, nx), lax.rem(me_x + nx - 1, nx)
    barrier = pltpu.get_barrier_semaphore()
    mesh_ids = pl.DeviceIdType.MESH

    def copy(k, source, target, axis, peer):
        return pltpu.make_async_remote_copy(
            src_ref=source, dst_ref=target, send_sem=send.at[k], recv_sem=recv.at[k],
            device_id={axis: peer}, device_id_type=mesh_ids,
        )

    first, final = pl.ds(0, BLOCK), pl.ds(cols - BLOCK, BLOCK)
    row_copies = [
        copy(0, volt.at[rows - 1], low, "gx", up),
        copy(1, volt.at[0], high, "gx", down),
        copy(2, cells.at[rows - 1], low_cells, "gx", up),
        copy(3, cells.at[0], high_cells, "gx", down),
    ]
    to_right = [
        copy(4, volt.at[:, final, :], left, "gy", me_y + 1),
        copy(5, cells.at[:, final, :], left_cells, "gy", me_y + 1),
    ]
    to_left = [
        copy(6, volt.at[:, first, :], right, "gy", me_y - 1),
        copy(7, cells.at[:, first, :], right_cells, "gy", me_y - 1),
    ]
    has_left, has_right = me_y > 0, me_y < ny - 1

    pl.semaphore_signal(barrier, inc=1, device_id={"gx": up}, device_id_type=mesh_ids)
    pl.semaphore_signal(barrier, inc=1, device_id={"gx": down}, device_id_type=mesh_ids)

    @pl.when(has_right)
    def _():
        pl.semaphore_signal(barrier, inc=1, device_id={"gy": me_y + 1}, device_id_type=mesh_ids)

    @pl.when(has_left)
    def _():
        pl.semaphore_signal(barrier, inc=1, device_id={"gy": me_y - 1}, device_id_type=mesh_ids)

    greeted = 2 + jnp.where(has_right, 1, 0) + jnp.where(has_left, 1, 0)
    pl.semaphore_wait(barrier, greeted)

    for c in row_copies:
        c.start()

    @pl.when(has_right)
    def _():
        for c in to_right:
            c.start()

    @pl.when(has_left)
    def _():
        for c in to_left:
            c.start()

    for c in row_copies:
        c.wait_recv()
        c.wait_send()

    @pl.when(has_right)
    def _():
        for c in to_right:
            c.wait_send()
        for c in to_left:
            c.wait_recv()

    @pl.when(has_left)
    def _():
        for c in to_left:
            c.wait_send()
        for c in to_right:
            c.wait_recv()


def body(volt, drive, region, diode_mask, sigma_table, cap_table):
    rows, cols, width = volt.shape
    regions = sigma_table.shape[0]
    nx, ny = lax.axis_size("gx"), lax.axis_size("gy")
    cells = jnp.concatenate(
        [
            lookup(region, sigma_table, regions),
            lookup(region, cap_table, regions),
            diode_mask.astype(jnp.float32),
            jnp.zeros((rows, cols, LANES - 3 * NZ), jnp.float32),
        ],
        axis=2,
    )
    anywhere = pl.BlockSpec(memory_space=pl.ANY)
    shaped = lambda *shape: jax.ShapeDtypeStruct(shape, jnp.float32)
    sides = (shaped(rows, BLOCK, width), shaped(rows, BLOCK, LANES))
    ends = (shaped(cols, width), shaped(cols, LANES))
    low, low_cells, high, high_cells, left, left_cells, right, right_cells = pl.pallas_call(
        functools.partial(halo_kernel, nx, ny, rows, cols),
        out_shape=ends * 2 + sides * 2,
        in_specs=[anywhere] * 2,
        out_specs=(anywhere,) * 8,
        scratch_shapes=[pltpu.SemaphoreType.DMA((8,)), pltpu.SemaphoreType.DMA((8,))],
        compiler_params=pltpu.CompilerParams(collective_id=1, has_side_effects=True),
        name="halos",
    )(volt, cells)
    forward, back = tables()

    whole = lambda *shape: pl.BlockSpec(shape, lambda i: (0,) * len(shape))
    row_spec = pl.BlockSpec((1, cols, width), lambda i: (i, 0, 0))
    side_spec = pl.BlockSpec((1, BLOCK, width), lambda i: (i, 0, 0))
    side_cells = pl.BlockSpec((1, BLOCK, LANES), lambda i: (i, 0, 0))
    residual, sums = pl.pallas_call(
        functools.partial(main_kernel, rows, cols),
        grid=(rows,),
        out_shape=(shaped(*volt.shape), shaped(8, LANES)),
        in_specs=[
            anywhere,
            anywhere,
            anywhere,
            row_spec,
            whole(rows, cols, LANES),
            whole(cols, LANES),
            whole(cols, LANES),
            side_spec,
            side_spec,
            side_cells,
            side_cells,
            whole(*forward.shape),
            whole(*back.shape),
        ],
        out_specs=(row_spec, whole(8, LANES)),
        scratch_shapes=[
            pltpu.VMEM((rows + 2, cols, width), jnp.float32),
            pltpu.VMEM((8, LANES), jnp.float32),
            pltpu.SemaphoreType.DMA((rows + 2,)),
        ],
        compiler_params=pltpu.CompilerParams(
            dimension_semantics=("arbitrary",), vmem_limit_bytes=50 * 2**20
        ),
        name="cells",
    )(
        volt, low, high, drive, cells, low_cells, high_cells,
        left, right, left_cells, right_cells, forward, back,
    )

    norms = pl.pallas_call(
        functools.partial(reduce_kernel, nx, ny, float(rows * cols * NZ * nx * ny)),
        out_shape=jax.ShapeDtypeStruct((8, LANES), jnp.float32),
        in_specs=[pl.BlockSpec(memory_space=pltpu.VMEM)],
        out_specs=pl.BlockSpec(memory_space=pltpu.VMEM),
        scratch_shapes=[
            pltpu.VMEM((nx, 8, LANES), jnp.float32),
            pltpu.VMEM((ny, 8, LANES), jnp.float32),
            pltpu.SemaphoreType.DMA((nx,)),
            pltpu.SemaphoreType.DMA((nx,)),
            pltpu.SemaphoreType.DMA((ny,)),
            pltpu.SemaphoreType.DMA((ny,)),
        ],
        compiler_params=pltpu.CompilerParams(collective_id=0, has_side_effects=True),
        name="norms",
    )(sums)
    return residual, norms[0, :KC]


def solution(mesh):
    return jax.shard_map(
        body,
        mesh=mesh,
        in_specs=(
            P("gx", "gy", None),
            P("gx", "gy", None),
            P("gx", "gy", None),
            P("gx", "gy", None),
            P(),
            P(),
        ),
        out_specs=(P("gx", "gy", None), P()),
        check_vma=False,
    )
```

time: 68 us -> 82.7 us (1.22)
  Pallas kernels: 43.3 us -> 55 us
  starting transfers between devices: 10.7 us -> 0 us
  other arithmetic: 3.19 us -> 12.6 us
  local copies, waits for them, and re-layouts: 9.37 us -> 13.5 us
    pallas_call x2, Pallas kernels: 31.1 us -> 44.1 us  [the longest x1 26.2 us: body(): pl.pallas_call(functools.partial(main_kernel, rows, cols), grid=(rows,),...]
    ppermute x4 -> x0, starting transfers between devices: 10.7 us -> none  [the longest x2 5.76 us: shift(): lax.ppermute(bottom, axis, backward)]
    select_n x0 -> x2, other arithmetic: none -> 10.7 us  [lookup(): value = jnp.where(region == r, table[r], value)]
    unnamed x18 -> x25, local copies, waits for them, and re-layouts: 2.02 us -> 8.89 us
    reduce_sum x3 -> x0, other arithmetic: 1.73 us -> none  [conduct_of(): value = jnp.sum(jnp.where(onehot, sigma_table, 0.0), axis=-1)]
    pallas_call x1, Pallas kernels: 12.3 us -> 10.9 us  [body(): pl.pallas_call(functools.partial(reduce_kernel, nx, ny, float(rows * cols...]
    convert_element_type x0 -> x1, other arithmetic: none -> 0.92 us  [body(): diode_mask.astype(jnp.float32)]
    reduce_sum x3 -> x0, local copies, waits for them, and re-layouts: 0.86 us -> none  [conduct_of(): value = jnp.sum(jnp.where(onehot, sigma_table, 0.0), axis=-1)]
  transfers between devices with their start and end apart: 4 -> 0, of which waited for: 0 -> 0; matrix products, arithmetic and copies ran while one was open for 10% -> 0% of each run, Pallas kernels for 37% -> 0%
where the time goes in v3:
time: 82.7 us; the launch traced here: 81.8 us
  Pallas kernels  55 us (67%)
  local copies, waits for them, and re-layouts  13.5 us (16%)
  other arithmetic  12.6 us (15%)
    pallas_call x1, Pallas kernels, body(): pl.pallas_call(functools.partial(main_kernel, rows, cols), grid=(rows,),...  26.2 us
    pallas_call x1, Pallas kernels, body(): pl.pallas_call(functools.partial(halo_kernel, nx, ny, rows, cols), out_sh...  17.9 us
    pallas_call x1, Pallas kernels, body(): pl.pallas_call(functools.partial(reduce_kernel, nx, ny, float(rows * cols...  10.9 us
    select_n x2, other arithmetic, lookup(): value = jnp.where(region == r, table[r], value)  10.7 us
    unnamed x25, local copies, waits for them, and re-layouts  8.89 us
    slice x2, local copies, waits for them, and re-layouts, lookup(): value = jnp.where(region == r, table[r], value)  3.26 us

profile of v3, /device:TPU:0, one launch (start us, length us, event | category | flops | bytes accessed | tf_op | source)
XLA Modules:
  0.0 81.8 jit_solution(2156812036666017178)
XLA Ops:
  0.6 1.6 %fusion.1 = (f32[1]{0:T(128)}, f32[1]{0:T(128)}, f32[1]{0:T(128)}, f32[1]{0:T(128)}, f32[1]{0:T(128)}, /*index=5*/f32[1]{0:T(128)}, f32[1]{0:T(128)}, f32[1]{0:T(128)}) fusion(f32[8]{0:T(128)} %param.12), kind=kLoop, calls=%fused_computation.13 | loop fusion | bytes 64 | tf_op jit(solution)/shard_map/slice | solution.py:52
  2.3 1.6 %fusion = (f32[1]{0:T(128)}, f32[1]{0:T(128)}, f32[1]{0:T(128)}, f32[1]{0:T(128)}, f32[1]{0:T(128)}, /*index=5*/f32[1]{0:T(128)}, f32[1]{0:T(128)}, f32[1]{0:T(128)}) fusion(f32[8]{0:T(128)} %param.13), kind=kLoop, calls=%fused_computation.12 | loop fusion | bytes 64 | tf_op jit(solution)/shard_map/slice | solution.py:52
  3.9 0.9 %convert_element_type.3 = f32[8,64,32]{1,2,0:T(8,128)S(1)} convert(s32[8,64,32]{1,2,0:T(8,128)} %param.11) | non-fusion elementwise | flops 16384 | bytes 131072 | tf_op jit(solution)/shard_map/convert_element_type | solution.py:318
  4.8 0.1 copy.27
  4.9 0.0 copy-start.1
  5.0 0.0 copy-start.6
  5.0 1.1 %copy.19 = s32[8,64,32]{2,1,0:T(8,128)S(1)} copy(s32[8,64,32]{1,2,0:T(8,128)} %param.10) | data formatting | bytes 131072 | tf_op args[2]
  6.1 5.4 %select_select_fusion.1 = (f32[8,64,32]{2,1,0:T(8,128)S(1)}, pred[8,64,32]{2,1,0:T(8,128)(4,1)S(1)}, pred[8,64,32]{2,1,0:T(8,128)(4,1)S(1)}, pred[8,64,32]{2,1,0...) fusion(f32[]{:T(128)} %bitcast.7, f32[]{:T(128)} %bitcast.6, ...), kind=kLoop, calls=%fused_computation.2 | loop fusion | flops 262144 | bytes 262176 | tf_op jit(solution)/shard_map/jit(_where)/select_n | solution.py:52
  11.5 5.3 %select_select_fusion = f32[8,64,32]{2,1,0:T(8,128)S(1)} fusion(pred[8,64,32]{2,1,0:T(8,128)(4,1)S(1)} %get-tuple-element.30, pred[8,64,32]{2,1,0:T(8,128)(4,1)S(1)} %get-tuple-element.29, pred[8,64,32]{2,1,0:T(8,128)(4,1)S(1)} %get-tuple-element.28, pred[8,64,32]{2,1,0:T(8,128)(4,1)S(1)} %get-tuple-element.27, pred[8,64,32]{2,1,0:T(8,128)(4,1)S(1)} %get-tuple-element.26, ...), kind=kLoop, calls=%fused_computation.1 | loop fusion | flops 131072 | bytes 196640 | tf_op jit(solution)/shard_map/jit(_where)/select_n | solution.py:52
  16.8 1.0 %pad_maximum_fusion.cells.cells_ref = f32[8,64,128]{2,1,0:T(8,128)} fusion(f32[8,64,32]{2,1,0:T(8,128)S(1)} %broadcast_in_dim.64, f32[8,64,32]{2,1,0:T(8,128)S(1)} %copy.27, f32[8,64,32]{2,1,0:T(8,128)S(1)} %select_select_fusion, f32[8,64,32]{2,1,0:T(8,128)S(1)} %get-tuple-element.22), kind=kLoop, calls=%fused_computation | loop fusion | flops 196608 | bytes 524288 | tf_op jit(solution)/shard_map/concatenate | solution.py:314
  17.8 0.0 copy-start
  17.8 17.9 %halos.1 = (f32[64,2048]{1,0:T(8,128)}, f32[64,128]{1,0:T(8,128)}, f32[64,2048]{1,0:T(8,128)}, f32[64,128]{1,0:T(8,128)}, f32[8,8,2048]{2,1,0:T(8,128)}, /*index...) custom-call(f32[8,64,2048]{2,1,0:T(8,128)} %volt_hbm.1, f32[8,64,128]{2,1,0:T(8,128)} %pad_maximum_fusion.cells.cells_ref), custom_call_target="tpu_custom_call" | custom-call | tf_op jit(solution)/shard_map/halos/pallas_call | solution.py:327
  35.7 0.0 copy-done.1
  35.7 0.0 copy-done.6
  35.7 0.0 copy-done
  35.7 0.0 copy-start.2
  35.7 1.0 %copy-done.2 = f32[64,2048]{1,0:T(8,128)S(1)} copy-done((f32[64,2048]{1,0:T(8,128)S(1)}, f32[64,2048]{1,0:T(8,128)}, u32[]{:S(2)}) %copy-start.2) | copy-done | bytes 524312
  36.8 0.0 copy-start.3
  36.8 1.0 %copy-done.3 = f32[64,2048]{1,0:T(8,128)S(1)} copy-done((f32[64,2048]{1,0:T(8,128)S(1)}, f32[64,2048]{1,0:T(8,128)}, u32[]{:S(2)}) %copy-start.3) | copy-done | bytes 524312
  37.8 0.0 copy-start.4
  37.8 1.0 %copy-done.4 = f32[8,8,2048]{2,1,0:T(8,128)S(1)} copy-done((f32[8,8,2048]{2,1,0:T(8,128)S(1)}, f32[8,8,2048]{2,1,0:T(8,128)}, u32[]{:S(2)}) %copy-start.4) | copy-done | bytes 524312
  38.8 0.0 copy-start.5
  38.9 1.0 %copy-done.5 = f32[8,8,2048]{2,1,0:T(8,128)S(1)} copy-done((f32[8,8,2048]{2,1,0:T(8,128)S(1)}, f32[8,8,2048]{2,1,0:T(8,128)}, u32[]{:S(2)}) %copy-start.5) | copy-done | bytes 524312
  39.9 0.8 copy-done.7
  40.7 0.8 copy-done.8
  41.4 0.8 copy-done.9
  42.2 0.8 copy-done.10
  42.9 26.2 %cells.1 = (f32[8,64,2048]{2,1,0:T(8,128)}, f32[8,128]{1,0:T(8,128)S(1)}) custom-call(f32[8,64,2048]{2,1,0:T(8,128)} %volt_hbm.1, f32[64,2048]{1,0:T(8,128)S(1)} %copy-done.2, f32[64,2048]{1,0:T(8,128)S(1)} %copy-done.3, f32[8,64,2048]{2,1,0:T(8,128)} %drive_ref.1, f32[8,64,128]{2,1,0:T(8,128)S(1)} %copy-done, f32[64,128]{1,0:T(8,128)S(1)} %copy-done.7, ...), custom_call_target="tpu_custom_call" | custom-call | tf_op jit(solution)/shard_map/cells/pallas_call | solution.py:342
  69.1 0.0 copy-start.11
  69.2 0.6 copy-done.11
  69.7 10.9 %norms.1 = f32[8,128]{1,0:T(8,128)} custom-call(f32[8,128]{1,0:T(8,128)} %copy-done.11), custom_call_target="tpu_custom_call" | custom-call | tf_op jit(solution)/shard_map/norms/pallas_call | solution.py:376
  80.6 1.2 %slice_bitcast_fusion = f32[64]{0:T(128)} fusion(f32[8,128]{1,0:T(8,128)} %norms.1), kind=kLoop, calls=%fused_computation.11 | loop fusion | bytes 512 | tf_op jit(solution)/shard_map/squeeze | solution.py:392
  (5 shorter events, 0.0 us)
Async XLA Ops:
  4.9 30.7 %copy-start.1 = (bf16[1024,256]{1,0:T(8,128)(2,1)S(1)}, bf16[1024,256]{1,0:T(8,128)(2,1)}, u32[]{:S(2)}) copy-start(bf16[1024,256]{1,0:T(8,128)(2,1)} %constant.24.clone.back_ref) | copy-start | bytes 1572868
  5.0 30.7 %copy-start.6 = (bf16[256,256]{1,0:T(8,128)(2,1)S(1)}, bf16[256,256]{1,0:T(8,128)(2,1)}, u32[]{:S(2)}) copy-start(bf16[256,256]{1,0:T(8,128)(2,1)} %constant.10.clone.forward_ref) | copy-start | bytes 393220
  17.8 17.9 %copy-start = (f32[8,64,128]{2,1,0:T(8,128)S(1)}, f32[8,64,128]{2,1,0:T(8,128)}, u32[]{:S(2)}) copy-start(f32[8,64,128]{2,1,0:T(8,128)} %pad_maximum_fusion.cells.cells_ref) | copy-start | bytes 786436
  35.7 1.0 %copy-start.2 = (f32[64,2048]{1,0:T(8,128)S(1)}, f32[64,2048]{1,0:T(8,128)}, u32[]{:S(2)}) copy-start(f32[64,2048]{1,0:T(8,128)} %get-tuple-element.12.low_hbm) | copy-start | bytes 1572868
  36.8 1.0 %copy-start.3 = (f32[64,2048]{1,0:T(8,128)S(1)}, f32[64,2048]{1,0:T(8,128)}, u32[]{:S(2)}) copy-start(f32[64,2048]{1,0:T(8,128)} %get-tuple-element.13.high_hbm) | copy-start | bytes 1572868
  37.8 1.0 %copy-start.4 = (f32[8,8,2048]{2,1,0:T(8,128)S(1)}, f32[8,8,2048]{2,1,0:T(8,128)}, u32[]{:S(2)}) copy-start(f32[8,8,2048]{2,1,0:T(8,128)} %get-tuple-element.16.left_ref) | copy-start | bytes 1572868
  38.8 1.0 %copy-start.5 = (f32[8,8,2048]{2,1,0:T(8,128)S(1)}, f32[8,8,2048]{2,1,0:T(8,128)}, u32[]{:S(2)}) copy-start(f32[8,8,2048]{2,1,0:T(8,128)} %get-tuple-element.17.right_ref) | copy-start | bytes 1572868
  39.9 0.8 copy-start.7
  40.6 0.8 copy-start.8
  41.4 0.8 copy-start.9
  42.2 0.8 copy-start.10
  69.1 0.6 copy-start.11

commit v4 on v3

--- a/solution.py
+++ b/solution.py
@@ -16,7 +16,6 @@
 LANES = 128
 TILES = NZ * KC // LANES
 CHUNK = 8
-BLOCK = 8
 
 base_freq = 0.1
 norm_eps = 1e-06
@@ -57,19 +56,19 @@
     return 2.0 * left * right / (left + right)
 
 
-def spread(cells, tile, lane, base=0):
-    index = base + 2 * tile + (lane >= KC).astype(jnp.int32)
+def spread(cells, tile, lane):
+    index = 2 * tile + (lane >= KC).astype(jnp.int32)
     return jnp.take_along_axis(cells, index, axis=1, mode="promise_in_bounds")
 
 
 def main_kernel(
-    rows, cols,
-    volt_hbm, low_hbm, high_hbm, drive_ref, cells_ref, low_cells, high_cells,
-    left_ref, right_ref, left_cells, right_cells, forward_ref, back_ref,
-    out_ref, squares_ref, volt_buf, acc_ref, sems,
+    rows, cols, regions,
+    volt_hbm, ends_hbm, drive_ref, region_ref, mask_ref, end_regions,
+    side_ref, side_regions, sigma_ref, cap_ref, forward_ref, back_ref,
+    out_ref, squares_ref, volt_buf, cond_buf, cell_buf, side_buf, acc_ref, sems,
 ):
     i = pl.program_id(0)
-    sources = [low_hbm] + [volt_hbm.at[row] for row in range(rows)] + [high_hbm]
+    sources = [ends_hbm.at[0]] + [volt_hbm.at[row] for row in range(rows)] + [ends_hbm.at[1]]
 
     def copy(slot):
         return pltpu.make_async_copy(sources[slot], volt_buf.at[slot], sems.at[slot])
@@ -79,6 +78,9 @@
         for slot in range(rows + 2):
             copy(slot).start()
         acc_ref[...] = jnp.zeros_like(acc_ref)
+        cond_buf[1 : rows + 1, :, :NZ] = lookup(region_ref[...], sigma_ref, regions)
+        cond_buf[0, :, :NZ] = lookup(end_regions[0], sigma_ref, regions)
+        cond_buf[rows + 1, :, :NZ] = lookup(end_regions[1], sigma_ref, regions)
         copy(0).wait()
         copy(1).wait()
 
@@ -90,17 +92,18 @@
 
     lane = lax.broadcasted_iota(jnp.int32, (cols, LANES), 1)
     col = lax.broadcasted_iota(jnp.int32, (cols, LANES), 0)
-    cells = cells_ref[i]
-    prev_cells = jnp.where(i > 0, cells_ref[jnp.maximum(i - 1, 0)], low_cells[...])
-    next_cells = jnp.where(
-        i < rows - 1, cells_ref[jnp.minimum(i + 1, rows - 1)], high_cells[...]
-    )
+    cell_buf[0, :, :NZ] = lookup(region_ref[i], cap_ref, regions)
+    cell_buf[1, :, :NZ] = mask_ref[i].astype(jnp.float32)
+    side_buf[0, :1, :NZ] = lookup(side_regions[0, 0], sigma_ref, regions)
+    side_buf[1, :1, :NZ] = lookup(side_regions[1, 0], sigma_ref, regions)
+    capacity, diode = cell_buf[0], cell_buf[1]
+    cells = cond_buf[i + 1]
     me, count = lax.axis_index("gy"), lax.axis_size("gy")
     has_left, has_right = me > 0, me < count - 1
-    g_low = harmonic_mean(cells, prev_cells)
-    g_high = harmonic_mean(cells, next_cells)
-    edge_left = jnp.where(has_left, left_cells[0, BLOCK - 1 :, :], 0.0)
-    edge_right = jnp.where(has_right, right_cells[0, :1, :], 0.0)
+    g_low = harmonic_mean(cells, cond_buf[i])
+    g_high = harmonic_mean(cells, cond_buf[i + 2])
+    edge_left = jnp.where(has_left, side_buf[0, :1], 0.0)
+    edge_right = jnp.where(has_right, side_buf[1, :1], 0.0)
     cells_after = jnp.where(
         col == cols - 1, jnp.broadcast_to(edge_right, cells.shape), pltpu.roll(cells, cols - 1, 0)
     )
@@ -151,12 +154,12 @@
             v = volt_buf[i + 1, :, at]
             value = spread(g_low, t, lane) * (v - volt_buf[i, :, at])
             value -= spread(g_high, t, lane) * (volt_buf[i + 2, :, at] - v)
-            right = jnp.where(has_right, right_ref[0, :1, at], 0.0)
+            right = jnp.where(has_right, side_ref[1, 0, :, at], 0.0)
             v_after = jnp.where(
                 col == cols - 1, jnp.broadcast_to(right, v.shape), pltpu.roll(v, cols - 1, 0)
             )
             col_flux = spread(g_col, t, lane) * (v_after - v)
-            left = jnp.where(has_left, left_ref[0, BLOCK - 1 :, at], 0.0)
+            left = jnp.where(has_left, side_ref[0, 0, :, at], 0.0)
             left_flux = spread(g_left, t, lane[:8]) * (v[:8] - jnp.broadcast_to(left, (8, LANES)))
             left_flux = jnp.concatenate([left_flux] * (cols // 8), axis=0)
             value += jnp.where(col == 0, left_flux, pltpu.roll(col_flux, 1, 0)) - col_flux
@@ -167,9 +170,9 @@
             value += jnp.where(first, before, deep_r) - deep_flux
             prev_flux = deep_r
             swapped = jnp.take_along_axis(v, swap, axis=1, mode="promise_in_bounds")
-            value += spread(cells, t, lane, NZ) * (order * swapped)
+            value += spread(capacity, t, lane) * (order * swapped)
             rows_of = slice((t - start) * cols, (t - start + 1) * cols)
-            value += spread(cells, t, lane, 2 * NZ) * (projected[rows_of] + 0.5 * v)
+            value += spread(diode, t, lane) * (projected[rows_of] + 0.5 * v)
             value -= drive_ref[0, :, at]
             out_ref[0, :, at] = value
             total += jnp.sum((value * value).reshape(cols // 8, 8, LANES), axis=0)
@@ -230,8 +233,7 @@
 
 
 def halo_kernel(
-    nx, ny, rows, cols, volt, cells,
-    low, low_cells, high, high_cells, left, left_cells, right, right_cells, send, recv,
+    nx, ny, rows, cols, volt, region, ends, end_regions, sides, side_regions, send, recv,
 ):
     me_x, me_y = lax.axis_index("gx"), lax.axis_index("gy")
     up, down = lax.rem(me_x + 1, nx), lax.rem(me_x + nx - 1, nx)
@@ -244,20 +246,20 @@
             device_id={axis: peer}, device_id_type=mesh_ids,
         )
 
-    first, final = pl.ds(0, BLOCK), pl.ds(cols - BLOCK, BLOCK)
+    first, final = pl.ds(0, 1), pl.ds(cols - 1, 1)
     row_copies = [
-        copy(0, volt.at[rows - 1], low, "gx", up),
-        copy(1, volt.at[0], high, "gx", down),
-        copy(2, cells.at[rows - 1], low_cells, "gx", up),
-        copy(3, cells.at[0], high_cells, "gx", down),
+        copy(0, volt.at[rows - 1], ends.at[0], "gx", up),
+        copy(1, volt.at[0], ends.at[1], "gx", down),
+        copy(2, region.at[rows - 1], end_regions.at[0], "gx", up),
+        copy(3, region.at[0], end_regions.at[1], "gx", down),
     ]
     to_right = [
-        copy(4, volt.at[:, final, :], left, "gy", me_y + 1),
-        copy(5, cells.at[:, final, :], left_cells, "gy", me_y + 1),
+        copy(4, volt.at[:, final, :], sides.at[0], "gy", me_y + 1),
+        copy(5, region.at[:, final, :], side_regions.at[0], "gy", me_y + 1),
     ]
     to_left = [
-        copy(6, volt.at[:, first, :], right, "gy", me_y - 1),
-        copy(7, cells.at[:, first, :], right_cells, "gy", me_y - 1),
+        copy(6, volt.at[:, first, :], sides.at[1], "gy", me_y - 1),
+        copy(7, region.at[:, first, :], side_regions.at[1], "gy", me_y - 1),
     ]
     has_left, has_right = me_y > 0, me_y < ny - 1
 
@@ -311,56 +313,52 @@
     rows, cols, width = volt.shape
     regions = sigma_table.shape[0]
     nx, ny = lax.axis_size("gx"), lax.axis_size("gy")
-    cells = jnp.concatenate(
-        [
-            lookup(region, sigma_table, regions),
-            lookup(region, cap_table, regions),
-            diode_mask.astype(jnp.float32),
-            jnp.zeros((rows, cols, LANES - 3 * NZ), jnp.float32),
-        ],
-        axis=2,
-    )
     anywhere = pl.BlockSpec(memory_space=pl.ANY)
     shaped = lambda *shape: jax.ShapeDtypeStruct(shape, jnp.float32)
-    sides = (shaped(rows, BLOCK, width), shaped(rows, BLOCK, LANES))
-    ends = (shaped(cols, width), shaped(cols, LANES))
-    low, low_cells, high, high_cells, left, left_cells, right, right_cells = pl.pallas_call(
+    ends, end_regions, sides, side_regions = pl.pallas_call(
         functools.partial(halo_kernel, nx, ny, rows, cols),
-        out_shape=ends * 2 + sides * 2,
+        out_shape=(
+            shaped(2, cols, width),
+            jax.ShapeDtypeStruct((2, cols, NZ), jnp.int32),
+            shaped(2, rows, 1, width),
+            jax.ShapeDtypeStruct((2, rows, 1, NZ), jnp.int32),
+        ),
         in_specs=[anywhere] * 2,
-        out_specs=(anywhere,) * 8,
+        out_specs=(anywhere,) * 4,
         scratch_shapes=[pltpu.SemaphoreType.DMA((8,)), pltpu.SemaphoreType.DMA((8,))],
         compiler_params=pltpu.CompilerParams(collective_id=1, has_side_effects=True),
         name="halos",
-    )(volt, cells)
+    )(volt, region)
     forward, back = tables()
 
     whole = lambda *shape: pl.BlockSpec(shape, lambda i: (0,) * len(shape))
     row_spec = pl.BlockSpec((1, cols, width), lambda i: (i, 0, 0))
-    side_spec = pl.BlockSpec((1, BLOCK, width), lambda i: (i, 0, 0))
-    side_cells = pl.BlockSpec((1, BLOCK, LANES), lambda i: (i, 0, 0))
+    side_map = lambda i: (0, i, 0, 0)
+    smem = pl.BlockSpec(memory_space=pltpu.SMEM)
     residual, sums = pl.pallas_call(
-        functools.partial(main_kernel, rows, cols),
+        functools.partial(main_kernel, rows, cols, regions),
         grid=(rows,),
         out_shape=(shaped(*volt.shape), shaped(8, LANES)),
         in_specs=[
             anywhere,
             anywhere,
-            anywhere,
             row_spec,
-            whole(rows, cols, LANES),
-            whole(cols, LANES),
-            whole(cols, LANES),
-            side_spec,
-            side_spec,
-            side_cells,
-            side_cells,
+            whole(rows, cols, NZ),
+            whole(rows, cols, NZ),
+            whole(2, cols, NZ),
+            pl.BlockSpec((2, 1, 1, width), side_map),
+            pl.BlockSpec((2, 1, 1, NZ), side_map),
+            smem,
+            smem,
             whole(*forward.shape),
             whole(*back.shape),
         ],
         out_specs=(row_spec, whole(8, LANES)),
         scratch_shapes=[
             pltpu.VMEM((rows + 2, cols, width), jnp.float32),
+            pltpu.VMEM((rows + 2, cols, LANES), jnp.float32),
+            pltpu.VMEM((2, cols, LANES), jnp.float32),
+            pltpu.VMEM((2, 8, LANES), jnp.float32),
             pltpu.VMEM((8, LANES), jnp.float32),
             pltpu.SemaphoreType.DMA((rows + 2,)),
         ],
@@ -369,8 +367,8 @@
         ),
         name="cells",
     )(
-        volt, low, high, drive, cells, low_cells, high_cells,
-        left, right, left_cells, right_cells, forward, back,
+        volt, ends, drive, region, diode_mask, end_regions, sides, side_regions,
+        sigma_table, cap_table, forward, back,
     )
 
     norms = pl.pallas_call(

time: 82.7 us -> 65.8 us (0.80)
  other arithmetic: 12.6 us -> 0 us
  local copies, waits for them, and re-layouts: 13.5 us -> 8.32 us
  Pallas kernels: 55 us -> 56.4 us
    select_n x2 -> x0, other arithmetic: 10.7 us -> none  [lookup(): value = jnp.where(region == r, table[r], value)]
    pallas_call x1, Pallas kernels: 10.9 us -> 14.3 us  [body(): pl.pallas_call(functools.partial(reduce_kernel, nx, ny, float(rows * cols...]
    pallas_call x1, Pallas kernels: 17.9 us -> 14.5 us  [body(): pl.pallas_call(functools.partial(halo_kernel, nx, ny, rows, cols), out_sh...]
    slice x2 -> x0, local copies, waits for them, and re-layouts: 3.26 us -> none  [lookup(): value = jnp.where(region == r, table[r], value)]
    unnamed x25 -> x22, local copies, waits for them, and re-layouts: 8.89 us -> 7.13 us
    pallas_call x1, Pallas kernels: 26.2 us -> 27.6 us  [body(): pl.pallas_call(functools.partial(main_kernel, rows, cols, regions), grid=...]
    concatenate x1 -> x0, other arithmetic: 0.98 us -> none  [body(): jnp.concatenate([lookup(region, sigma_table, regions), lookup(region, cap...]
    convert_element_type x1 -> x0, other arithmetic: 0.92 us -> none  [body(): diode_mask.astype(jnp.float32)]
where the time goes in v4:
time: 65.8 us; the launch traced here: 65.5 us
  Pallas kernels  56.4 us (86%)
  local copies, waits for them, and re-layouts  8.32 us (13%)
  between operations  0.75 us (1%)
    pallas_call x1, Pallas kernels, body(): pl.pallas_call(functools.partial(main_kernel, rows, cols, regions), grid=...  27.6 us
    pallas_call x1, Pallas kernels, body(): pl.pallas_call(functools.partial(halo_kernel, nx, ny, rows, cols), out_sh...  14.5 us
    pallas_call x1, Pallas kernels, body(): pl.pallas_call(functools.partial(reduce_kernel, nx, ny, float(rows * cols...  14.3 us
    unnamed x22, local copies, waits for them, and re-layouts  7.13 us

profile of v4, /device:TPU:0, one launch (start us, length us, event | category | flops | bytes accessed | tf_op | source)
XLA Modules:
  0.0 65.5 jit_solution(10212824184171786683)
XLA Ops:
  0.6 0.0 copy-start.2
  0.6 0.0 copy-start.3
  0.7 0.0 copy-start.9
  0.7 0.0 copy-start.8
  0.7 1.8 %copy.10.region.region_ref = s32[8,64,32]{2,1,0:T(8,128)} copy(s32[8,64,32]{1,2,0:T(8,128)} %param.10) | data formatting | bytes 131072 | tf_op args[2]
  2.5 0.0 copy-start
  2.5 1.1 %copy.12.mask_ref = s32[8,64,32]{2,1,0:T(8,128)S(1)} copy(s32[8,64,32]{1,2,0:T(8,128)} %param.11) | data formatting | bytes 131072 | tf_op args[3]
  3.6 14.5 %halos.1 = (f32[2,64,2048]{2,1,0:T(8,128)}, s32[2,64,32]{2,1,0:T(8,128)}, f32[2,8,1,2048]{3,2,1,0:T(1,128)}, s32[2,8,1,32]{3,2,1,0:T(1,128)}) custom-call(f32[8,64,2048]{2,1,0:T(8,128)} %volt_hbm.1, s32[8,64,32]{2,1,0:T(8,128)} %copy.10.region.region_ref), custom_call_target="tpu_custom_call" | custom-call | tf_op jit(solution)/shard_map/halos/pallas_call | solution.py:318
  18.1 0.0 copy-done.2
  18.1 0.0 copy-done.3
  18.1 0.0 copy-done.9
  18.1 0.0 copy-done.8
  18.1 0.0 copy-done
  18.1 0.0 copy-start.1
  18.2 1.2 %copy-done.1 = f32[2,64,2048]{2,1,0:T(8,128)S(1)} copy-done((f32[2,64,2048]{2,1,0:T(8,128)S(1)}, f32[2,64,2048]{2,1,0:T(8,128)}, u32[]{:S(2)}) %copy-start.1) | copy-done | bytes 1048600
  19.4 0.0 copy-start.4
  19.4 0.9 %copy-done.4 = f32[2,8,1,2048]{3,2,1,0:T(1,128)S(1)} copy-done((f32[2,8,1,2048]{3,2,1,0:T(1,128)S(1)}, f32[2,8,1,2048]{3,2,1,0:T(1,128)}, u32[]{:S(2)}) %copy-start.4) | copy-done | bytes 131096
  20.3 0.0 copy-start.5
  20.3 0.8 %copy-done.5 = s32[2,64,32]{2,1,0:T(8,128)S(1)} copy-done((s32[2,64,32]{2,1,0:T(8,128)S(1)}, s32[2,64,32]{2,1,0:T(8,128)}, u32[]{:S(2)}) %copy-start.5) | copy-done | bytes 16408
  21.1 0.0 copy-start.6
  21.1 0.7 %copy-done.6 = s32[2,8,1,32]{3,2,1,0:T(1,128)S(1)} copy-done((s32[2,8,1,32]{3,2,1,0:T(1,128)S(1)}, s32[2,8,1,32]{3,2,1,0:T(1,128)}, u32[]{:S(2)}) %copy-start.6) | copy-done | bytes 2072
  21.8 27.6 %cells.1 = (f32[8,64,2048]{2,1,0:T(8,128)}, f32[8,128]{1,0:T(8,128)S(1)}) custom-call(f32[8,64,2048]{2,1,0:T(8,128)} %volt_hbm.1, f32[2,64,2048]{2,1,0:T(8,128)S(1)} %copy-done.1, f32[8,64,2048]{2,1,0:T(8,128)} %drive_ref.1, s32[8,64,32]{2,1,0:T(8,128)S(1)} %copy-done, s32[8,64,32]{2,1,0:T(8,128)S(1)} %copy.12.mask_ref, s32[2,64,32]{2,1,0:T(8,128)S(1)} %copy-done.5, ...), custom_call_target="tpu_custom_call" | custom-call | tf_op jit(solution)/shard_map/cells/pallas_call | solution.py:338
  49.4 0.0 copy-start.7
  49.4 0.6 copy-done.7
  50.0 14.3 %norms.1 = f32[8,128]{1,0:T(8,128)} custom-call(f32[8,128]{1,0:T(8,128)} %copy-done.7), custom_call_target="tpu_custom_call" | custom-call | tf_op jit(solution)/shard_map/norms/pallas_call | solution.py:374
  64.3 1.2 %slice_bitcast_fusion = f32[64]{0:T(128)} fusion(f32[8,128]{1,0:T(8,128)} %norms.1), kind=kLoop, calls=%fused_computation | loop fusion | bytes 512 | tf_op jit(solution)/shard_map/squeeze | solution.py:390
Async XLA Ops:
  0.6 17.5 %copy-start.2 = (bf16[1024,256]{1,0:T(8,128)(2,1)S(1)}, bf16[1024,256]{1,0:T(8,128)(2,1)}, u32[]{:S(2)}) copy-start(bf16[1024,256]{1,0:T(8,128)(2,1)} %constant.5.clone.back_ref) | copy-start | bytes 1572868
  0.6 17.5 %copy-start.3 = (bf16[256,256]{1,0:T(8,128)(2,1)S(1)}, bf16[256,256]{1,0:T(8,128)(2,1)}, u32[]{:S(2)}) copy-start(bf16[256,256]{1,0:T(8,128)(2,1)} %constant.4.clone.forward_ref) | copy-start | bytes 393220
  0.7 17.5 %copy-start.9 = (f32[8]{0:T(128)S(1)}, f32[8]{0:T(128)}, u32[]{:S(2)}) copy-start(f32[8]{0:T(128)} %cap_ref.1) | copy-start | bytes 100
  0.7 17.5 %copy-start.8 = (f32[8]{0:T(128)S(1)}, f32[8]{0:T(128)}, u32[]{:S(2)}) copy-start(f32[8]{0:T(128)} %sigma_ref.1) | copy-start | bytes 100
  2.5 15.7 %copy-start = (s32[8,64,32]{2,1,0:T(8,128)S(1)}, s32[8,64,32]{2,1,0:T(8,128)}, u32[]{:S(2)}) copy-start(s32[8,64,32]{2,1,0:T(8,128)} %copy.10.region.region_ref) | copy-start | bytes 196612
  18.1 1.2 %copy-start.1 = (f32[2,64,2048]{2,1,0:T(8,128)S(1)}, f32[2,64,2048]{2,1,0:T(8,128)}, u32[]{:S(2)}) copy-start(f32[2,64,2048]{2,1,0:T(8,128)} %get-tuple-element.8.ends_hbm) | copy-start | bytes 3145732
  19.4 0.9 %copy-start.4 = (f32[2,8,1,2048]{3,2,1,0:T(1,128)S(1)}, f32[2,8,1,2048]{3,2,1,0:T(1,128)}, u32[]{:S(2)}) copy-start(f32[2,8,1,2048]{3,2,1,0:T(1,128)} %get-tuple-element.10.side_ref) | copy-start | bytes 393220
  20.3 0.8 %copy-start.5 = (s32[2,64,32]{2,1,0:T(8,128)S(1)}, s32[2,64,32]{2,1,0:T(8,128)}, u32[]{:S(2)}) copy-start(s32[2,64,32]{2,1,0:T(8,128)} %get-tuple-element.9.end_regions) | copy-start | bytes 49156
  21.1 0.7 %copy-start.6 = (s32[2,8,1,32]{3,2,1,0:T(1,128)S(1)}, s32[2,8,1,32]{3,2,1,0:T(1,128)}, u32[]{:S(2)}) copy-start(s32[2,8,1,32]{3,2,1,0:T(1,128)} %get-tuple-element.11.side_regions) | copy-start | bytes 6148
  49.4 0.6 copy-start.7

commit v5 on v4

--- a/solution.py
+++ b/solution.py
@@ -215,7 +215,7 @@
 
 
 def norm_of(total, cells):
-    value = jnp.broadcast_to(jnp.sum(total, axis=0, keepdims=True), total.shape)
+    value = jnp.broadcast_to(total, (8, LANES))
     value = value + pltpu.roll(value, KC, 1)
     return jnp.sqrt(value / cells + norm_eps)
 
@@ -224,7 +224,7 @@
     me_x, me_y = lax.axis_index("gx"), lax.axis_index("gy")
     greet("gx", nx, me_x)
     greet("gy", ny, me_y)
-    got_x[me_x] = in_ref[...]
+    got_x[me_x] = jnp.sum(in_ref[...], axis=0, keepdims=True)
     pl.semaphore_wait(pltpu.get_barrier_semaphore(), nx + ny - 2)
     exchange("gx", nx, me_x, got_x, send_x, recv_x)
     got_y[me_y] = jnp.sum(got_x[...], axis=0)
@@ -377,8 +377,8 @@
         in_specs=[pl.BlockSpec(memory_space=pltpu.VMEM)],
         out_specs=pl.BlockSpec(memory_space=pltpu.VMEM),
         scratch_shapes=[
-            pltpu.VMEM((nx, 8, LANES), jnp.float32),
-            pltpu.VMEM((ny, 8, LANES), jnp.float32),
+            pltpu.VMEM((nx, 1, LANES), jnp.float32),
+            pltpu.VMEM((ny, 1, LANES), jnp.float32),
             pltpu.SemaphoreType.DMA((nx,)),
             pltpu.SemaphoreType.DMA((nx,)),
             pltpu.SemaphoreType.DMA((ny,)),

time: 65.8 us -> 65.4 us (level)
  no operation moved by 1% of the time
where the time goes in v5:
time: 65.4 us; the launch traced here: 65 us
  Pallas kernels  56 us (86%)
  local copies, waits for them, and re-layouts  8.32 us (13%)
  between operations  0.75 us (1%)
    pallas_call x1, Pallas kernels, body(): pl.pallas_call(functools.partial(main_kernel, rows, cols, regions), grid=...  27.6 us
    pallas_call x1, Pallas kernels, body(): pl.pallas_call(functools.partial(halo_kernel, nx, ny, rows, cols), out_sh...  14.5 us
    pallas_call x1, Pallas kernels, body(): pl.pallas_call(functools.partial(reduce_kernel, nx, ny, float(rows * cols...  13.9 us
    unnamed x22, local copies, waits for them, and re-layouts  7.13 us

profile of v5, /device:TPU:0, one launch (start us, length us, event | category | flops | bytes accessed | tf_op | source)
XLA Modules:
  0.0 65.0 jit_solution(8359191785003581124)
XLA Ops:
  0.6 0.0 copy-start.2
  0.6 0.0 copy-start.3
  0.7 0.0 copy-start.9
  0.7 0.0 copy-start.8
  0.7 1.8 %copy.10.region.region_ref = s32[8,64,32]{2,1,0:T(8,128)} copy(s32[8,64,32]{1,2,0:T(8,128)} %param.10) | data formatting | bytes 131072 | tf_op args[2]
  2.5 0.0 copy-start
  2.5 1.1 %copy.12.mask_ref = s32[8,64,32]{2,1,0:T(8,128)S(1)} copy(s32[8,64,32]{1,2,0:T(8,128)} %param.11) | data formatting | bytes 131072 | tf_op args[3]
  3.6 14.5 %halos.1 = (f32[2,64,2048]{2,1,0:T(8,128)}, s32[2,64,32]{2,1,0:T(8,128)}, f32[2,8,1,2048]{3,2,1,0:T(1,128)}, s32[2,8,1,32]{3,2,1,0:T(1,128)}) custom-call(f32[8,64,2048]{2,1,0:T(8,128)} %volt_hbm.1, s32[8,64,32]{2,1,0:T(8,128)} %copy.10.region.region_ref), custom_call_target="tpu_custom_call" | custom-call | tf_op jit(solution)/shard_map/halos/pallas_call | solution.py:318
  18.1 0.0 copy-done.2
  18.1 0.0 copy-done.3
  18.1 0.0 copy-done.9
  18.1 0.0 copy-done.8
  18.1 0.0 copy-done
  18.1 0.0 copy-start.1
  18.2 1.2 %copy-done.1 = f32[2,64,2048]{2,1,0:T(8,128)S(1)} copy-done((f32[2,64,2048]{2,1,0:T(8,128)S(1)}, f32[2,64,2048]{2,1,0:T(8,128)}, u32[]{:S(2)}) %copy-start.1) | copy-done | bytes 1048600
  19.4 0.0 copy-start.4
  19.4 0.9 %copy-done.4 = f32[2,8,1,2048]{3,2,1,0:T(1,128)S(1)} copy-done((f32[2,8,1,2048]{3,2,1,0:T(1,128)S(1)}, f32[2,8,1,2048]{3,2,1,0:T(1,128)}, u32[]{:S(2)}) %copy-start.4) | copy-done | bytes 131096
  20.3 0.0 copy-start.5
  20.3 0.8 %copy-done.5 = s32[2,64,32]{2,1,0:T(8,128)S(1)} copy-done((s32[2,64,32]{2,1,0:T(8,128)S(1)}, s32[2,64,32]{2,1,0:T(8,128)}, u32[]{:S(2)}) %copy-start.5) | copy-done | bytes 16408
  21.1 0.0 copy-start.6
  21.1 0.7 %copy-done.6 = s32[2,8,1,32]{3,2,1,0:T(1,128)S(1)} copy-done((s32[2,8,1,32]{3,2,1,0:T(1,128)S(1)}, s32[2,8,1,32]{3,2,1,0:T(1,128)}, u32[]{:S(2)}) %copy-start.6) | copy-done | bytes 2072
  21.8 27.6 %cells.1 = (f32[8,64,2048]{2,1,0:T(8,128)}, f32[8,128]{1,0:T(8,128)S(1)}) custom-call(f32[8,64,2048]{2,1,0:T(8,128)} %volt_hbm.1, f32[2,64,2048]{2,1,0:T(8,128)S(1)} %copy-done.1, f32[8,64,2048]{2,1,0:T(8,128)} %drive_ref.1, s32[8,64,32]{2,1,0:T(8,128)S(1)} %copy-done, s32[8,64,32]{2,1,0:T(8,128)S(1)} %copy.12.mask_ref, s32[2,64,32]{2,1,0:T(8,128)S(1)} %copy-done.5, ...), custom_call_target="tpu_custom_call" | custom-call | tf_op jit(solution)/shard_map/cells/pallas_call | solution.py:338
  49.4 0.0 copy-start.7
  49.4 0.6 copy-done.7
  50.0 13.9 %norms.1 = f32[8,128]{1,0:T(8,128)} custom-call(f32[8,128]{1,0:T(8,128)} %copy-done.7), custom_call_target="tpu_custom_call" | custom-call | tf_op jit(solution)/shard_map/norms/pallas_call | solution.py:374
  63.8 1.2 %slice_bitcast_fusion = f32[64]{0:T(128)} fusion(f32[8,128]{1,0:T(8,128)} %norms.1), kind=kLoop, calls=%fused_computation | loop fusion | bytes 512 | tf_op jit(solution)/shard_map/squeeze | solution.py:390
Async XLA Ops:
  0.6 17.5 %copy-start.2 = (bf16[1024,256]{1,0:T(8,128)(2,1)S(1)}, bf16[1024,256]{1,0:T(8,128)(2,1)}, u32[]{:S(2)}) copy-start(bf16[1024,256]{1,0:T(8,128)(2,1)} %constant.5.clone.back_ref) | copy-start | bytes 1572868
  0.6 17.5 %copy-start.3 = (bf16[256,256]{1,0:T(8,128)(2,1)S(1)}, bf16[256,256]{1,0:T(8,128)(2,1)}, u32[]{:S(2)}) copy-start(bf16[256,256]{1,0:T(8,128)(2,1)} %constant.4.clone.forward_ref) | copy-start | bytes 393220
  0.7 17.5 %copy-start.9 = (f32[8]{0:T(128)S(1)}, f32[8]{0:T(128)}, u32[]{:S(2)}) copy-start(f32[8]{0:T(128)} %cap_ref.1) | copy-start | bytes 100
  0.7 17.5 %copy-start.8 = (f32[8]{0:T(128)S(1)}, f32[8]{0:T(128)}, u32[]{:S(2)}) copy-start(f32[8]{0:T(128)} %sigma_ref.1) | copy-start | bytes 100
  2.5 15.7 %copy-start = (s32[8,64,32]{2,1,0:T(8,128)S(1)}, s32[8,64,32]{2,1,0:T(8,128)}, u32[]{:S(2)}) copy-start(s32[8,64,32]{2,1,0:T(8,128)} %copy.10.region.region_ref) | copy-start | bytes 196612
  18.1 1.2 %copy-start.1 = (f32[2,64,2048]{2,1,0:T(8,128)S(1)}, f32[2,64,2048]{2,1,0:T(8,128)}, u32[]{:S(2)}) copy-start(f32[2,64,2048]{2,1,0:T(8,128)} %get-tuple-element.8.ends_hbm) | copy-start | bytes 3145732
  19.4 0.9 %copy-start.4 = (f32[2,8,1,2048]{3,2,1,0:T(1,128)S(1)}, f32[2,8,1,2048]{3,2,1,0:T(1,128)}, u32[]{:S(2)}) copy-start(f32[2,8,1,2048]{3,2,1,0:T(1,128)} %get-tuple-element.10.side_ref) | copy-start | bytes 393220
  20.3 0.8 %copy-start.5 = (s32[2,64,32]{2,1,0:T(8,128)S(1)}, s32[2,64,32]{2,1,0:T(8,128)}, u32[]{:S(2)}) copy-start(s32[2,64,32]{2,1,0:T(8,128)} %get-tuple-element.9.end_regions) | copy-start | bytes 49156
  21.1 0.7 %copy-start.6 = (s32[2,8,1,32]{3,2,1,0:T(1,128)S(1)}, s32[2,8,1,32]{3,2,1,0:T(1,128)}, u32[]{:S(2)}) copy-start(s32[2,8,1,32]{3,2,1,0:T(1,128)} %get-tuple-element.11.side_regions) | copy-start | bytes 6148
  49.4 0.6 copy-start.7
